TPU v7x, 128 devices: a whole 4x4x4 slice. The times are simulated.
128 devices in a mesh: model: 64 (over z, y, x), data: 2 (over core).
Axes of the slice: x: 4, y: 4, z: 4, core: 2. Of those that a mesh axis runs over, the one named last changes fastest.
Arguments:
- tokens: bfloat16 [16384, 1664], P('data')
- w_up: bfloat16 [1664, 8192], P(None, 'model')
- w_down: bfloat16 [8192, 1664], P('model')
- task_heads: bfloat16 [8, 1664, 2], replicated
- labels: int32 [8, 16384], P(None, 'data')
Outputs:
- output 1: float32 [8], replicated
- output 2: float32 [1664, 8192], P('data', 'model')
- output 3: float32 [8192, 1664], P(('model', 'data'))
All inputs are finite; a program needn't handle non-finite values.
Results may differ from a plain program's by a relative error of at most 0.001.
Values are sent between devices in bfloat16 or wider.
A program may use at most 1 GiB of HBM per device.

v0:
```python
import jax
import jax.numpy as jnp
from jax import lax
from jax.sharding import PartitionSpec as P

STEPS = 20


def simplex_weights(gram_mat):
    n_task = gram_mat.shape[0]
    trace_scale = jnp.trace(gram_mat) / n_task

    def eg_step(step_idx, weights):
        updated = weights * jnp.exp(-jnp.sum(gram_mat * weights[None, :], axis=1) / trace_scale)
        return updated / jnp.sum(updated)

    return lax.fori_loop(0, STEPS, eg_step, jnp.full((n_task,), 1.0 / n_task, jnp.float32))


def solution(mesh):
    n_data = mesh.shape['data']

    def local_step(tokens, w_up, w_down, task_heads, labels):
        n_total = tokens.shape[0] * n_data
        n_class = task_heads.shape[2]
        pre_act = jnp.dot(tokens, w_up, preferred_element_type=jnp.float32)
        act_val, gelu_slope = jax.jvp(jax.nn.gelu, (pre_act,), (jnp.ones_like(pre_act),))
        act_bf = act_val.astype(jnp.bfloat16)
        part_out = jnp.dot(act_bf, w_down, preferred_element_type=jnp.float32)
        mlp_out = lax.psum(part_out, 'model')
        trunk_out = (tokens.astype(jnp.float32) + mlp_out).astype(jnp.bfloat16)
        logits = jnp.einsum('bd,tdc->tbc', trunk_out, task_heads, preferred_element_type=jnp.float32)
        class_prob = jax.nn.softmax(logits, axis=-1)
        onehot = jax.nn.one_hot(labels, n_class, dtype=jnp.float32)
        dlogit = (class_prob - onehot) / n_total
        d_trunk = jnp.einsum('tbc,tdc->tbd', dlogit, task_heads.astype(jnp.float32), precision=lax.Precision.HIGHEST).astype(jnp.bfloat16)
        g_down = jnp.einsum('bf,tbd->tfd', act_bf, d_trunk, preferred_element_type=jnp.float32)
        d_act = jnp.einsum('tbd,fd->tbf', d_trunk, w_down, preferred_element_type=jnp.float32)
        d_pre = (d_act * gelu_slope[None]).astype(jnp.bfloat16)
        g_up = jnp.einsum('bd,tbf->tdf', tokens, d_pre, preferred_element_type=jnp.float32)
        up_shard = lax.psum_scatter(g_up, 'data', scatter_dimension=1, tiled=True)
        down_shard = lax.psum_scatter(g_down, 'data', scatter_dimension=1, tiled=True)
        gram_part = (jnp.einsum('tij,sij->ts', up_shard, up_shard, precision=lax.Precision.HIGHEST)
                     + jnp.einsum('tij,sij->ts', down_shard, down_shard, precision=lax.Precision.HIGHEST))
        gram_mat = lax.psum(gram_part, ('model', 'data'))
        task_weights = simplex_weights(gram_mat)
        grad_up = jnp.einsum('t,tij->ij', task_weights, up_shard, precision=lax.Precision.HIGHEST)
        grad_down = jnp.einsum('t,tij->ij', task_weights, down_shard, precision=lax.Precision.HIGHEST)
        return task_weights, grad_up, grad_down

    return jax.shard_map(
        local_step, mesh=mesh,
        in_specs=(P('data', None), P(None, 'model'), P('model', None), P(None, None, None), P(None, 'data')),
        out_specs=(P(None), P('data', 'model'), P(('model', 'data'), None)),
        check_vma=False)
```

profile of v0, /device:TPU:1, one launch (start us, length us, event | category | flops | bytes accessed | tf_op | source)
XLA Modules:
  0.0 1096.6 jit_solution(9890334587232567787)
XLA Ops:
  7.2 16.0 %fusion.23 = (f32[8192,128]{1,0:T(8,128)}, f32[8192,128]{1,0:T(8,128)}) fusion(bf16[8192,1664]{1,0:T(8,128)(2,1)} %param.7, bf16[1664,128]{1,0:T(8,128)(2,1)} %param.8), kind=kOutput, calls=%fused_computation.27 | convolution fusion | flops 3506438144 | bytes 36077568 | tf_op jit(solution)/shard_map/dot_general | solution.py:26
  23.2 22.5 %fusion.36 = f32[8192,1664]{1,0:T(8,128)} fusion(bf16[128,1664]{1,0:T(8,128)(2,1)S(1)} %copy-done, f32[8192,128]{1,0:T(8,128)} %get-tuple-element.54), kind=kOutput, calls=%fused_computation.48 | convolution fusion | flops 3499098112 | bytes 59146240 | tf_op jit(solution)/shard_map/dot_general | solution.py:29
  45.8 5.7 copy.18
  51.5 465.1 %all-reduce.2.cloned.1.call-done = f32[8192,1664]{1,0:T(8,128)} async-done(((f32[8192,1664]{1,0:T(8,128)}), f32[8192,1664]{1,0:T(8,128)}) %all-reduce.2.cloned.1.call-update) | async-done | bytes 54525968 | tf_op jit(solution)/shard_map/psum | solution.py:30
  516.6 26.4 %fusion.38 = (f32[8,8192]{1,0:T(8,128)S(1)}, f32[8,8192,2]{1,0,2:T(8,128)S(1)}) fusion(bf16[8,1664,2]{1,2,0:T(2,128)(2,1)S(1)} %copy-done.3, f32[8192,1664]{1,0:T(8,128)} %all-reduce.2.cloned.1.call-done, bf16[8192,1664]{1,0:T(8,128)(2,1)} %param.7), kind=kOutput, calls=%fused_computation.50 | convolution fusion | flops 477167616 | bytes 82628608 | tf_op jit(solution)/shard_map/bd,tdc->tbc/dot_general | solution.py:32
  543.2 192.9 %convolution_convert_fusion = bf16[8,8192,1664]{2,1,0:T(8,128)(2,1)} fusion(bf16[8,1664,2]{1,2,0:T(2,128)(2,1)S(1)} %copy-done.3, f32[8,8192,2]{1,0,2:T(8,128)S(1)} %subtract_multiply_fusion), kind=kOutput, calls=%fused_computation.4 | convolution fusion | flops 2726297600 | bytes 218681344 | tf_op jit(solution)/shard_map/tbc,tdc->tbd/dot_general | solution.py:36
  736.2 80.7 %convolution_bitcast_fusion = f32[8,128,1664]{1,2,0:T(8,128)} fusion(bf16[8,8192,1664]{2,1,0:T(8,128)(2,1)} %convolution_convert_fusion, f32[8192,128]{1,0:T(8,128)} %get-tuple-element.54), kind=kOutput, calls=%fused_computation.17 | convolution fusion | flops 27926724608 | bytes 229113856 | tf_op jit(solution)/shard_map/bf,tbd->tfd/dot_general | solution.py:37
  816.9 7.8 copy.21
  824.7 83.7 %multiply_convert_fusion.9 = bf16[8,8192,128]{1,2,0:T(8,128)(2,1)} fusion(bf16[8,8192,1664]{2,1,0:T(8,128)(2,1)} %convolution_convert_fusion, f32[8192,128]{0,1:T(8,128)} %copy.18, bf16[128,1664]{1,0:T(8,128)(2,1)S(1)} %copy-done), kind=kOutput, calls=%fused_computation.6.clone.clone.clone.clone.1 | convolution fusion | flops 27934064640 | bytes 239501312 | tf_op jit(solution)/shard_map/tbd,fd->tbf/dot_general | solution.py:38
  908.4 38.0 %fusion.11 = f32[8,1664,128]{1,2,0:T(8,128)} fusion(bf16[8192,1664]{1,0:T(8,128)(2,1)} %param.7, bf16[8,8192,128]{1,2,0:T(8,128)(2,1)} %multiply_convert_fusion.9), kind=kOutput, calls=%fused_computation.16 | convolution fusion | flops 27917287424 | bytes 50855936 | tf_op jit(solution)/shard_map/bd,tbf->tdf/dot_general | solution.py:40
  946.5 7.8 copy.19
  954.4 10.6 convolution_bitcast_fusion.1
  965.0 7.9 reduce-scatter.3.cloned.1.call-done
  972.9 10.6 fusion.27
  983.5 66.8 %psum.15 = f32[8,8]{1,0:T(8,128)S(1)} all-reduce(f32[8,8]{1,0:T(8,128)S(1)} %fusion.27), channel_id=1, replica_groups=mesh['model'=64,'data'=2] {'model','data'}, use_global_device_ids=true, to_apply=%region_5.6 | all-reduce | flops 64 | bytes 512 | tf_op jit(solution)/shard_map/psum | solution.py:45
  1051.6 28.4 %while.11 = (s32[]{:T(128)}, f32[8]{0:T(128)S(1)}, f32[8,8]{1,0:T(8,128)S(1)}, f32[]{:T(128)}, s32[]{:T(128)}, /*index=5*/s32[]{:T(128)}) while((s32[]{:T(128)}, f32[8]{0:T(128)S(1)}, f32[8,8]{1,0:T(8,128)S(1)}, f32[]{:T(128)}, s32[]{:T(128)}, /*index=5*/s32[]{:T(128)}) %tuple.31), condition=%wide.region_10.11_spmd.clone, body=%wide.region_7.10_spmd.clone.sunk | while | flops 178 | bytes 636 | solution.py:17
  1052.3 0.6 broadcast_divide_fusion.2
  1053.8 0.6 broadcast_divide_fusion.2
  1056.6 0.6 broadcast_divide_fusion.2
  1058.0 0.6 broadcast_divide_fusion.2
  1060.9 0.6 broadcast_divide_fusion.2
  1080.0 5.0 fusion.33
  1085.0 0.8 copy.31
  1085.8 3.8 fusion.24
  (96 shorter events, 25.6 us)
Async XLA Ops:
  7.2 16.0 %copy-start = (bf16[128,1664]{1,0:T(8,128)(2,1)S(1)}, bf16[128,1664]{1,0:T(8,128)(2,1)}, u32[]{:S(2)}) copy-start(bf16[128,1664]{1,0:T(8,128)(2,1)} %param.9) | copy-start | bytes 1277956
  7.2 509.4 %all-reduce.2.cloned.1.call-start = ((), (), s32[]{:S(2)}) async-start(), calls=%async_computation.2 | async-start | bytes 109051904 | tf_op jit(solution)/shard_map/psum | solution.py:30
  45.8 908.6 %reduce-scatter.5.cloned.1.call-start = ((), (), s32[]{:S(2)}) async-start(), calls=%async_computation.4 | async-start | bytes 10223616 | tf_op jit(solution)/shard_map/reduce_scatter | solution.py:42
  45.8 470.8 %copy-start.3 = (bf16[8,1664,2]{1,2,0:T(2,128)(2,1)S(1)}, bf16[8,1664,2]{1,2,0:T(2,128)(2,1)}, u32[]{:S(2)}) copy-start(bf16[8,1664,2]{1,2,0:T(2,128)(2,1)} %param.10) | copy-start | bytes 159748
  51.5 491.6 %copy-start.2 = (s32[8,8192]{1,0:T(8,128)S(1)}, s32[8,8192]{1,0:T(8,128)}, u32[]{:S(2)}) copy-start(s32[8,8192]{1,0:T(8,128)} %param.11) | copy-start | bytes 786436
  824.7 148.3 %reduce-scatter.3.cloned.1.call-start = ((), (), s32[]{:S(2)}) async-start(), calls=%async_computation.3 | async-start | bytes 10223616 | tf_op jit(solution)/shard_map/reduce_scatter | solution.py:41
  1080.0 9.7 copy-start.4
  1080.0 5.8 copy-start.1
Sparse Core Ops, SparseCore 0:
  45.9 470.6 all-reduce.1
  824.8 18.4 reduce-scatter.4
  954.5 18.4 reduce-scatter.2
where the time goes:
time: 1100 us
  matrix products  490 us (45%)
  waiting for transfers between devices  473 us (43%)
  blocking collectives  66.8 us (6%)
  other arithmetic  28.6 us (3%)
  local copies, waits for them, and re-layouts  22.1 us (2%)
  between operations  14.9 us (1%)
    psum x1, waiting for transfers between devices, local_step(): mlp_out = lax.psum(part_out, 'model')  465 us
    dot_general x1, matrix products, local_step(): jnp.einsum('tbc,tdc->tbd', dlogit, task_heads.astype(jnp.float32), precis...  193 us
    dot_general x1, matrix products, local_step(): jnp.einsum('tbd,fd->tbf', d_trunk, w_down, preferred_element_type=jnp.flo...  83.7 us
    dot_general x1, matrix products, local_step(): jnp.einsum('bf,tbd->tfd', act_bf, d_trunk, preferred_element_type=jnp.flo...  80.7 us
    psum x1, blocking collectives, local_step(): gram_mat = lax.psum(gram_part, ('model', 'data'))  66.8 us
    dot_general x1, matrix products, local_step(): jnp.einsum('bd,tbf->tdf', tokens, d_pre, preferred_element_type=jnp.float32)  38 us
    dot_general x1, matrix products, local_step(): jnp.einsum('bd,tdc->tbc', trunk_out, task_heads, preferred_element_type=j...  26.4 us
    dot_general x1, matrix products, local_step(): part_out = jnp.dot(act_bf, w_down, preferred_element_type=jnp.float32)  22.5 us
  transfers between devices with their start and end apart: 3, of which 2 were waited for; matrix products, arithmetic and copies ran while one was open for 13% of the time, Pallas kernels for 0%

commit v1 on v0

v1 whole, which is shorter than its diff:
```python
import functools

import jax
import jax.numpy as jnp
from jax import lax
from jax.experimental import pallas as pl
from jax.experimental.pallas import tpu as pltpu
from jax.sharding import PartitionSpec as P

STEPS = 20
LANES = 128
MESH = pl.DeviceIdType.MESH
F32 = jnp.float32
BF16 = jnp.bfloat16
C_GELU = 0.7978845608028654
K_GELU = 0.044715
NT = (((1,), (1,)), ((), ()))


def peer(model, data):
    return {"model": model, "data": data}


def ring_barrier(n_model, me_d, pair):
    sem = pltpu.get_barrier_semaphore()
    me = lax.axis_index("model")

    def tell(k, carry):
        pl.semaphore_signal(sem, inc=1, device_id=peer(lax.rem(me + k, n_model), me_d), device_id_type=MESH)
        return carry

    lax.fori_loop(1, n_model, tell, 0)
    if pair:
        pl.semaphore_signal(sem, inc=1, device_id=peer(me, 1 - me_d), device_id_type=MESH)
    return sem, n_model - 1 + (1 if pair else 0)


def forward_kernel(n_model, tile, win, x_ref, w1t_ref, ut_ref, gpt_ref, u2_ref, xz_ref,
                   xbuf, usend, xsem, send_sem, recv_sem, pair_sem):
    me = lax.axis_index("model")
    core = lax.axis_index("data")
    n_tok = x_ref.shape[0]
    blk = n_tok // n_model
    n_tile = n_tok // tile
    per = tile // blk
    off = x_ref.shape[1] - win
    sem, count = ring_barrier(n_model, core, True)
    start = lax.div(me, per)

    def tile_at(i):
        return lax.rem(i + start, n_tile)

    def fetch(i, slot):
        rows = pl.ds(pl.multiple_of(tile_at(i) * tile, tile), tile)
        return pltpu.make_async_copy(x_ref.at[rows, :], xbuf.at[slot], xsem.at[slot])

    fetch(0, 0).start()
    pl.semaphore_wait(sem, count)
    mine = pl.ds(pl.multiple_of(me * blk, blk), blk)
    own_x = pltpu.make_async_copy(x_ref.at[mine, pl.ds(pl.multiple_of(core * off, LANES), win)],
                                  xz_ref.at[pl.ds(0, blk), :], pair_sem.at[0])
    own_x.start()
    far_x = pltpu.make_async_remote_copy(
        src_ref=x_ref.at[mine, pl.ds(pl.multiple_of((1 - core) * off, LANES), win)],
        dst_ref=xz_ref.at[pl.ds(blk, blk), :], send_sem=pair_sem.at[1], recv_sem=pair_sem.at[2],
        device_id=peer(me, 1 - core), device_id_type=MESH)
    far_x.start()

    def step(i, carry):
        slot = lax.rem(i, 2)

        @pl.when(i + 1 < n_tile)
        def _():
            fetch(i + 1, 1 - slot).start()

        fetch(i, slot).wait()
        base = pl.multiple_of(tile_at(i) * tile, tile)
        a = lax.dot_general(w1t_ref[...], xbuf[slot], NT, preferred_element_type=F32)
        a2 = a * a
        th = jnp.tanh(C_GELU * (a + K_GELU * (a * a2)))
        cdf = 0.5 * (1.0 + th)
        slope = cdf + a * (0.5 * (1.0 - th * th) * (C_GELU * (1.0 + (3.0 * K_GELU) * a2)))
        u_f = a * cdf
        ut_ref[:, pl.ds(base, tile)] = u_f.astype(BF16)
        gpt_ref[:, pl.ds(base, tile)] = slope
        usend[pl.ds(base, tile), :] = u_f.T.astype(BF16)
        dst = u2_ref.at[pl.ds(0, blk), pl.ds(pl.multiple_of(me * LANES, LANES), LANES)]
        for k in range(per):
            src = usend.at[pl.ds(pl.multiple_of(base + k * blk, blk), blk), :]
            owner = tile_at(i) * per + k

            @pl.when(owner != me)
            def _():
                pltpu.make_async_remote_copy(
                    src_ref=src, dst_ref=dst, send_sem=send_sem, recv_sem=recv_sem,
                    device_id=peer(owner, core), device_id_type=MESH).start()

            @pl.when(owner == me)
            def _():
                pltpu.make_async_copy(src, dst, recv_sem).start()
        return carry

    lax.fori_loop(0, n_tile, step, 0)
    own_u = u2_ref.at[pl.ds(0, blk), :]
    pltpu.make_async_copy(own_u, own_u, recv_sem).wait()
    far_u = pltpu.make_async_remote_copy(
        src_ref=own_u, dst_ref=u2_ref.at[pl.ds(blk, blk), :], send_sem=pair_sem.at[3], recv_sem=pair_sem.at[4],
        device_id=peer(me, 1 - core), device_id_type=MESH)
    far_u.start()
    sent = usend.at[pl.ds(0, n_tok - blk), :]
    pltpu.make_async_copy(sent, sent, send_sem).wait()
    own_x.wait()
    far_x.wait()
    far_u.wait()


def token_kernel(n_model, chunk, n_total, u2_ref, w2g_ref, xz_ref, ht_ref, lab_ref, et_ref,
                 wbuf, acc, lsend, lrecv, esend, wsem, pair_sem, send_sem, recv_sem):
    me = lax.axis_index("model")
    core = lax.axis_index("data")
    blk = u2_ref.shape[0] // 2
    n_chunk = w2g_ref.shape[0] // chunk
    n_task = lab_ref.shape[0]
    sem, count = ring_barrier(n_model, core, True)

    def fetch(i, slot):
        rows = pl.ds(pl.multiple_of(i * chunk, chunk), chunk)
        return pltpu.make_async_copy(w2g_ref.at[rows, :], wbuf.at[slot], wsem.at[slot])

    fetch(0, 0).start()
    fetch(1, 1).start()
    acc[...] = xz_ref[...].astype(F32) * 0.0

    def step(i, carry):
        slot = lax.rem(i, 3)

        @pl.when(i + 2 < n_chunk)
        def _():
            fetch(i + 2, lax.rem(i + 2, 3)).start()

        fetch(i, slot).wait()
        cols = pl.ds(pl.multiple_of(i * chunk, chunk), chunk)
        acc[...] += jnp.dot(u2_ref[:, cols], wbuf[slot], preferred_element_type=F32)
        return carry

    lax.fori_loop(0, n_chunk, step, 0)
    z = (xz_ref[...].astype(F32) + acc[...]).astype(BF16)
    part = lax.dot_general(ht_ref[...], z, NT, preferred_element_type=F32)
    lsend[...] = part[:, blk:]
    pl.semaphore_wait(sem, count)
    swap = pltpu.make_async_remote_copy(
        src_ref=lsend, dst_ref=lrecv, send_sem=pair_sem.at[0], recv_sem=pair_sem.at[1],
        device_id=peer(me, 1 - core), device_id_type=MESH)
    swap.start()
    swap.wait()
    logit = part[:, :blk] + lrecv[...]
    gap = logit[:n_task, :] - logit[n_task:, :]
    first = lab_ref[...] == 0
    wrong = 1.0 / (1.0 + jnp.exp(jnp.where(first, gap, -gap)))
    esend[...] = jnp.where(first, -wrong, wrong) * (1.0 / n_total)

    dst = et_ref.at[:, pl.ds(pl.multiple_of(me * blk, LANES), blk)]

    def send(k, carry):
        pltpu.make_async_remote_copy(
            src_ref=esend, dst_ref=dst, send_sem=send_sem, recv_sem=recv_sem,
            device_id=peer(lax.rem(me + k, n_model), core), device_id_type=MESH).start()
        return carry

    lax.fori_loop(1, n_model, send, 0)
    pltpu.make_async_copy(esend, dst, recv_sem).start()
    pltpu.make_async_copy(et_ref, et_ref, recv_sem).wait()
    sent = et_ref.at[:, pl.ds(0, (n_model - 1) * blk)]
    pltpu.make_async_copy(sent, sent, send_sem).wait()


def grad_kernel(et_ref, ut_ref, gpt_ref, x_ref, w2_ref, drow_ref, dcol_ref, gdn_ref, gup_ref,
                dn_acc, up_acc, ebr, dat, out_sem):
    step = pl.program_id(0)
    n_task, tile = et_ref.shape
    width, hidden = w2_ref.shape
    wide = 256
    cuts = [(c, min(wide, hidden - c)) for c in range(0, hidden, wide)]

    @pl.when(step == 0)
    def _():
        dn_acc[...] = jnp.zeros_like(dn_acc)
        up_acc[...] = jnp.zeros_like(up_acc)

    for t in range(n_task):
        ebr[t] = et_ref[t:t + 1, :]

    def one_task(t, carry):
        e_row = ebr[t]
        for n in range(0, tile, wide):
            e_n = e_row[:, n:n + wide]
            da = jnp.zeros((width, wide), F32)
            for c, size in cuts:
                d_c = dcol_ref[t, c:c + size, :]
                d_c = jnp.concatenate([d_c] * (wide // LANES), axis=1)
                dz_t = (d_c * e_n).astype(BF16)
                da = da + jnp.dot(w2_ref[:, c:c + size], dz_t, preferred_element_type=F32)
            dat[pl.ds(pl.multiple_of(t * width, width), width), n:n + wide] = (da * gpt_ref[:, n:n + wide]).astype(BF16)
        e_col = jnp.broadcast_to(e_row, (LANES, tile)).T
        for c, size in cuts:
            e_b = e_col
            e_b = jnp.concatenate([e_b] * (size // LANES), axis=1)
            dz = (e_b * drow_ref[t, :, c:c + size]).astype(BF16)
            dn_acc[t, :, c:c + size] += jnp.dot(ut_ref[...], dz, preferred_element_type=F32)
        return carry

    lax.fori_loop(0, n_task, one_task, 0)
    rows = 2 * width

    def up_part(m, carry):
        at = pl.ds(pl.multiple_of(m * rows, rows), rows)
        left = dat[at, :]
        for c, size in cuts:
            up_acc[at, c:c + size] += jnp.dot(left, x_ref[:, c:c + size], preferred_element_type=F32)
        return carry

    lax.fori_loop(0, n_task * width // rows, up_part, 0)

    @pl.when(step == pl.num_programs(0) - 1)
    def _():
        one = pltpu.make_async_copy(dn_acc, gdn_ref, out_sem.at[0])
        two = pltpu.make_async_copy(up_acc, gup_ref, out_sem.at[1])
        one.start()
        two.start()
        one.wait()
        two.wait()


def mix_kernel(n_model, win, gdn_ref, gup_ref, a_ref, g1_ref, g2_ref,
               dn_own, dn_far, up_own, up_far, msend, mrecv, g1t, dsem, usem, send_sem, recv_sem):
    me = lax.axis_index("model")
    core = lax.axis_index("data")
    n_task, half, hidden = dn_own.shape
    width = 2 * half
    off = hidden - win
    sem = pltpu.get_barrier_semaphore()

    n_all = 2 * n_model
    slot = me * 2 + core

    def other(k):
        at = lax.rem(slot + k, n_all)
        return peer(lax.div(at, 2), lax.rem(at, 2))

    def tell(k, carry):
        pl.semaphore_signal(sem, inc=1, device_id=other(k), device_id_type=MESH)
        return carry

    lax.fori_loop(1, n_all, tell, 0)
    my_cols = pl.ds(pl.multiple_of(core * off, LANES), win)
    far_cols = pl.ds(pl.multiple_of((1 - core) * off, LANES), win)
    local = []
    for t in range(n_task):
        local.append(pltpu.make_async_copy(
            gdn_ref.at[t, pl.ds(pl.multiple_of(core * half, half), half), :], dn_own.at[t], dsem.at[0, t]))
        local.append(pltpu.make_async_copy(
            gup_ref.at[pl.ds(t * width, width), my_cols], up_own.at[t], usem.at[0, t]))
    for c in local:
        c.start()
    pl.semaphore_wait(sem, n_all - 1)
    far = []
    for t in range(n_task):
        far.append(pltpu.make_async_remote_copy(
            src_ref=gdn_ref.at[t, pl.ds(pl.multiple_of((1 - core) * half, half), half), :], dst_ref=dn_far.at[t],
            send_sem=dsem.at[1, t], recv_sem=dsem.at[2, t], device_id=peer(me, 1 - core), device_id_type=MESH))
        far.append(pltpu.make_async_remote_copy(
            src_ref=gup_ref.at[pl.ds(t * width, width), far_cols], dst_ref=up_far.at[t],
            send_sem=usem.at[1, t], recv_sem=usem.at[2, t], device_id=peer(me, 1 - core), device_id_type=MESH))
    for c in far:
        c.start()
    for c in local:
        c.wait()
    for c in far:
        c.wait()

    pairs = [(t, s) for t in range(n_task) for s in range(t, n_task)]
    lane = lax.broadcasted_iota(jnp.int32, (8, LANES), 1)

    def fold(own, other, r, c, keep, sums):
        rows = pl.ds(pl.multiple_of(r * 8, 8), 8)
        vals = []
        for t in range(n_task):
            v = own[t, rows, c:c + LANES] + other[t, rows, c:c + LANES]
            own[t, rows, c:c + LANES] = v
            vals.append(v if keep is None else jnp.where(keep, v, 0.0))
        return tuple(acc + vals[t] * vals[s] for acc, (t, s) in zip(sums, pairs))

    sums = tuple(jnp.zeros((8, LANES), F32) for _ in pairs)
    for c in range(0, hidden, LANES):
        sums = lax.fori_loop(0, half // 8, functools.partial(
            lambda c, r, s: fold(dn_own, dn_far, r, c, None, s), c), sums)
    first = core * (win - hidden // 2)
    for c in range(0, win, LANES):
        edge = c < win - hidden // 2 or c + LANES > hidden // 2
        keep = (lane + c >= first) & (lane + c < first + hidden // 2) if edge else None
        sums = lax.fori_loop(0, width // 8, functools.partial(
            lambda c, keep, r, s: fold(up_own, up_far, r, c, keep, s), c, keep), sums)

    row = lax.broadcasted_iota(jnp.int32, (8, LANES), 0)
    part = jnp.zeros((8, LANES), F32)
    for acc, (t, s) in zip(sums, pairs):
        total = jnp.sum(jnp.sum(acc, axis=1, keepdims=True), axis=0, keepdims=True)
        here = ((row == t) & (lane == s)) | ((row == s) & (lane == t))
        part = part + jnp.where(here, total, 0.0)
    msend[...] = part

    def send(k, carry):
        pltpu.make_async_remote_copy(
            src_ref=msend, dst_ref=mrecv.at[slot], send_sem=send_sem, recv_sem=recv_sem,
            device_id=other(k), device_id_type=MESH).start()
        return carry

    lax.fori_loop(1, n_all, send, 0)
    pltpu.make_async_copy(msend, mrecv.at[slot], recv_sem).start()
    pltpu.make_async_copy(mrecv, mrecv, recv_sem).wait()
    gram = jnp.sum(mrecv[...], axis=0)

    scale = jnp.sum(jnp.sum(jnp.where(row == lane, gram, 0.0), axis=1, keepdims=True), axis=0, keepdims=True) / n_task
    gram = gram / scale
    w = jnp.where(lane < n_task, 1.0 / n_task, 0.0).astype(F32)

    def eg_pair(i, w):
        v = w[:, 0:1] * 0.0 + jnp.sum(gram * w, axis=1, keepdims=True)
        w_col = jnp.sum(jnp.where(row == lane, w, 0.0), axis=1, keepdims=True)
        w_col = w_col * jnp.exp(-v)
        w_col = w_col / jnp.sum(w_col, axis=0, keepdims=True)
        v = jnp.sum(gram * w_col, axis=0, keepdims=True)
        w_row = jnp.sum(jnp.where(row == lane, w_col, 0.0), axis=0, keepdims=True)
        w_row = w_row * jnp.exp(-v)
        w_row = w_row / jnp.sum(w_row, axis=1, keepdims=True)
        return jnp.broadcast_to(w_row, (8, LANES))

    w = lax.fori_loop(0, STEPS // 2, eg_pair, w)
    a_ref[...] = w
    a = [jnp.sum(jnp.where(lane == t, w, 0.0), axis=1, keepdims=True) for t in range(n_task)]

    for c in range(0, hidden, LANES):
        def body2(r, carry, c=c):
            rows = pl.ds(pl.multiple_of(r * 8, 8), 8)
            total = a[0] * dn_own[0, rows, c:c + LANES]
            for t in range(1, n_task):
                total = total + a[t] * dn_own[t, rows, c:c + LANES]
            g2_ref[rows, c:c + LANES] = total
            return carry
        lax.fori_loop(0, half // 8, body2, 0)
    for c in range(0, win, LANES):
        def body1(r, carry, c=c):
            rows = pl.ds(pl.multiple_of(r * 8, 8), 8)
            total = a[0] * up_own[0, rows, c:c + LANES]
            for t in range(1, n_task):
                total = total + a[t] * up_own[t, rows, c:c + LANES]
            up_far[0, rows, c:c + LANES] = total
            return carry
        lax.fori_loop(0, width // 8, body1, 0)
    for c in range(0, win, LANES):
        g1t[c:c + LANES, :] = up_far[0, :, c:c + LANES].T
    g1_ref[...] = g1t[pl.ds(pl.multiple_of(first, 8), hidden // 2), :]
    sent = mrecv.at[pl.ds(0, n_all - 1)]
    pltpu.make_async_copy(sent, sent, send_sem).wait()


def solution(mesh):
    n_model, n_data = mesh.shape['model'], mesh.shape['data']

    def local_step(tokens, w_up, w_down, task_heads, labels):
        n_tok, hidden = tokens.shape
        n_total = n_tok * n_data
        width = w_up.shape[1]
        n_task = task_heads.shape[0]
        blk = n_tok // n_model
        win = -(-(hidden // 2) // LANES) * LANES
        off = hidden - win
        me = lax.axis_index('model')
        core = lax.axis_index('data')
        any_spec = pl.BlockSpec(memory_space=pl.ANY)
        vmem_spec = pl.BlockSpec(memory_space=pltpu.VMEM)
        big = 60 * 1024 * 1024

        w2_win = lax.dynamic_slice(w_down, (0, core * off), (width, win))
        w2_all = lax.all_gather(w2_win, 'model', axis=0, tiled=True)

        tile = min(512, n_tok)
        ut, gpt, u2, xz = pl.pallas_call(
            functools.partial(forward_kernel, n_model, tile, win),
            out_shape=(jax.ShapeDtypeStruct((width, n_tok), BF16), jax.ShapeDtypeStruct((width, n_tok), F32),
                       jax.ShapeDtypeStruct((2 * blk, n_model * width), BF16),
                       jax.ShapeDtypeStruct((2 * blk, win), BF16)),
            in_specs=[any_spec, vmem_spec],
            out_specs=(vmem_spec, vmem_spec, any_spec, any_spec),
            scratch_shapes=[pltpu.VMEM((2, tile, hidden), BF16), pltpu.VMEM((n_tok, width), BF16),
                            pltpu.SemaphoreType.DMA((2,)), pltpu.SemaphoreType.DMA, pltpu.SemaphoreType.DMA,
                            pltpu.SemaphoreType.DMA((5,))],
            compiler_params=pltpu.CompilerParams(collective_id=0, has_side_effects=True, vmem_limit_bytes=big),
            cost_estimate=pl.CostEstimate(flops=4 * n_tok * hidden * width, bytes_accessed=n_tok * hidden * 2,
                                          transcendentals=n_tok * width),
            name='forward_send')(tokens, w_up.T)

        heads = task_heads.astype(F32)
        h_t = jnp.concatenate([task_heads[:, :, 0], task_heads[:, :, 1]], axis=0)
        h_win = lax.dynamic_slice(h_t, (0, core * off), (2 * n_task, win))
        col = lax.broadcasted_iota(jnp.int32, (2 * n_task, win), 1)
        edge = core * (win - hidden // 2)
        h_win = jnp.where((col >= edge) & (col < edge + hidden // 2), h_win, jnp.zeros_like(h_win))
        my_lab = lax.dynamic_slice(labels, (0, me * blk), (n_task, blk))
        chunk = min(512, n_model * width)
        e_t = pl.pallas_call(
            functools.partial(token_kernel, n_model, chunk, n_total),
            out_shape=jax.ShapeDtypeStruct((n_task, n_tok), F32),
            in_specs=[vmem_spec, any_spec, vmem_spec, vmem_spec, vmem_spec],
            out_specs=vmem_spec,
            scratch_shapes=[pltpu.VMEM((3, chunk, win), BF16), pltpu.VMEM((2 * blk, win), F32),
                            pltpu.VMEM((2 * n_task, blk), F32), pltpu.VMEM((2 * n_task, blk), F32),
                            pltpu.VMEM((n_task, blk), F32), pltpu.SemaphoreType.DMA((3,)),
                            pltpu.SemaphoreType.DMA((2,)), pltpu.SemaphoreType.DMA, pltpu.SemaphoreType.DMA],
            compiler_params=pltpu.CompilerParams(collective_id=1, has_side_effects=True, vmem_limit_bytes=big),
            cost_estimate=pl.CostEstimate(flops=2 * n_tok * hidden * width, bytes_accessed=n_model * width * win * 2,
                                          transcendentals=0),
            name='token_side')(u2, w2_all, xz, h_win, my_lab)

        d_row = heads[:, :, 0] - heads[:, :, 1]
        d_col = jnp.broadcast_to(d_row[:, :, None], (n_task, hidden, LANES))
        t_b = min(512, n_tok)
        const2 = lambda i: (0, 0)
        g_dn, g_up = pl.pallas_call(
            grad_kernel,
            out_shape=(jax.ShapeDtypeStruct((n_task, width, hidden), F32),
                       jax.ShapeDtypeStruct((n_task * width, hidden), F32)),
            grid=(n_tok // t_b,),
            in_specs=[pl.BlockSpec((n_task, t_b), lambda i: (0, i)), pl.BlockSpec((width, t_b), lambda i: (0, i)),
                      pl.BlockSpec((width, t_b), lambda i: (0, i)), pl.BlockSpec((t_b, hidden), lambda i: (i, 0)),
                      pl.BlockSpec((width, hidden), const2, pipeline_mode=pl.Buffered(1)),
                      pl.BlockSpec((n_task, 1, hidden), lambda i: (0, 0, 0), pipeline_mode=pl.Buffered(1)),
                      pl.BlockSpec((n_task, hidden, LANES), lambda i: (0, 0, 0), pipeline_mode=pl.Buffered(1))],
            out_specs=(any_spec, any_spec),
            scratch_shapes=[pltpu.VMEM((n_task, width, hidden), F32), pltpu.VMEM((n_task * width, hidden), F32),
                            pltpu.VMEM((n_task, 1, t_b), F32),
                            pltpu.VMEM((n_task * width, t_b), BF16),
                            pltpu.SemaphoreType.DMA((2,))],
            compiler_params=pltpu.CompilerParams(dimension_semantics=('arbitrary',), vmem_limit_bytes=big),
            cost_estimate=pl.CostEstimate(flops=48 * n_tok * hidden * width, bytes_accessed=n_tok * hidden * 2,
                                          transcendentals=0),
            name='task_grads')(e_t, ut, gpt, tokens, w_down, d_row[:, None, :], d_col)

        half = width // 2
        weights, grad_up, grad_down = pl.pallas_call(
            functools.partial(mix_kernel, n_model, win),
            out_shape=(jax.ShapeDtypeStruct((8, LANES), F32), jax.ShapeDtypeStruct((hidden // 2, width), F32),
                       jax.ShapeDtypeStruct((half, hidden), F32)),
            in_specs=[any_spec, any_spec],
            out_specs=(vmem_spec, vmem_spec, vmem_spec),
            scratch_shapes=[pltpu.VMEM((n_task, half, hidden), F32), pltpu.VMEM((n_task, half, hidden), F32),
                            pltpu.VMEM((n_task, width, win), F32), pltpu.VMEM((n_task, width, win), F32),
                            pltpu.VMEM((8, LANES), F32), pltpu.VMEM((2 * n_model, 8, LANES), F32),
                            pltpu.VMEM((win, width), F32),
                            pltpu.SemaphoreType.DMA((3, n_task)), pltpu.SemaphoreType.DMA((3, n_task)),
                            pltpu.SemaphoreType.DMA, pltpu.SemaphoreType.DMA],
            compiler_params=pltpu.CompilerParams(collective_id=2, has_side_effects=True, vmem_limit_bytes=big),
            name='mix')(g_dn, g_up)
        return weights[0, :n_task], grad_up, grad_down

    return jax.shard_map(
        local_step, mesh=mesh,
        in_specs=(P('data', None), P(None, 'model'), P('model', None), P(None, None, None), P(None, 'data')),
        out_specs=(P(None), P('data', 'model'), P(('model', 'data'), None)),
        check_vma=False)
```

time: 1100 us -> 346 us (0.31)
  matrix products: 490 us -> 0 us
  waiting for transfers between devices: 473 us -> 59.8 us
  Pallas kernels: 0 us -> 255 us
  blocking collectives: 66.8 us -> 0 us
  other arithmetic: 28.6 us -> 2.2 us
    dot_general x10 -> x0, matrix products: 487 us -> none  [the longest x1 193 us: local_step(): jnp.einsum('tbc,tdc->tbd', dlogit, task_heads.astype(jnp.float32), precis...]
    psum x1 -> x0, waiting for transfers between devices: 465 us -> none  [local_step(): mlp_out = lax.psum(part_out, 'model')]
    pallas_call x0 -> x4, Pallas kernels: none -> 255 us  [the longest x1 139 us: local_step(): pl.pallas_call(grad_kernel, out_shape=(jax.ShapeDtypeStruct((n_task, widt...]
    psum x1 -> x0, blocking collectives: 66.8 us -> none  [local_step(): gram_mat = lax.psum(gram_part, ('model', 'data'))]
    all_gather x0 -> x1, waiting for transfers between devices: none -> 59.8 us  [local_step(): w2_all = lax.all_gather(w2_win, 'model', axis=0, tiled=True)]
    transpose x2 -> x0, local copies, waits for them, and re-layouts: 15.6 us -> none  [the longest x1 7.85 us: local_step(): jnp.einsum('bd,tbf->tdf', tokens, d_pre, preferred_element_type=jnp.float32)]
    reduce_sum x42 -> x0, other arithmetic: 15.4 us -> none  [the longest x20 12.4 us: eg_step(): return updated / jnp.sum(updated)]
    div x21 -> x0, other arithmetic: 13.1 us -> none  [the longest x20 13 us: eg_step(): return updated / jnp.sum(updated)]
  transfers between devices with their start and end apart: 3 -> 1, of which waited for: 2 -> 1; matrix products, arithmetic and copies ran while one was open for 13% -> 2% of each run, Pallas kernels for 0% -> 15%
where the time goes in v1:
time: 346 us; the launch traced here: 345 us
  Pallas kernels  255 us (74%)
  waiting for transfers between devices  59.8 us (17%)
  local copies, waits for them, and re-layouts  14.1 us (4%)
  between operations  14.1 us (4%)
    pallas_call x1, Pallas kernels, local_step(): pl.pallas_call(grad_kernel, out_shape=(jax.ShapeDtypeStruct((n_task, widt...  139 us
    all_gather x1, waiting for transfers between devices, local_step(): w2_all = lax.all_gather(w2_win, 'model', axis=0, tiled=True)  59.8 us
    pallas_call x1, Pallas kernels, local_step(): pl.pallas_call(functools.partial(forward_kernel, n_model, tile, win), out...  53 us
    pallas_call x1, Pallas kernels, local_step(): pl.pallas_call(functools.partial(mix_kernel, n_model, win), out_shape=(ja...  38.8 us
    pallas_call x1, Pallas kernels, local_step(): pl.pallas_call(functools.partial(token_kernel, n_model, chunk, n_total),...  24.2 us
  transfers between devices with their start and end apart: 1, of which 1 were waited for; matrix products, arithmetic and copies ran while one was open for 2% of the time, Pallas kernels for 15%

profile of v1, /device:TPU:1, one launch (start us, length us, event | category | flops | bytes accessed | tf_op | source)
XLA Modules:
  0.0 345.0 jit_solution(18171011751346114957)
XLA Ops:
  7.2 0.0 copy-start
  7.2 0.0 all-gather.2.cloned.1.call-start
  7.2 1.7 constant_dynamic-slice_fusion.1
  8.9 0.0 all-gather.2.cloned.1.call-update
  8.9 2.0 copy.8
  10.9 0.8 convert_element_type.3
  11.8 0.1 slice_subtract_fusion
  11.9 0.0 copy-done
  11.9 0.6 constant_dynamic-slice_fusion.lab_ref
  12.5 1.0 fusion.3
  13.5 0.6 fusion.1.ht_ref
  14.1 0.7 fusion.4.drow_ref
  14.8 53.0 %forward_send.1 = (bf16[128,8192]{1,0:T(8,128)(2,1)}, f32[128,8192]{1,0:T(8,128)}, bf16[256,8192]{1,0:T(8,128)(2,1)}, bf16[256,896]{1,0:T(8,128)(2,1)}) custom-call(bf16[8192,1664]{1,0:T(8,128)(2,1)} %x_ref.3, bf16[128,1664]{1,0:T(8,128)(2,1)} %bitcast.12), custom_call_target="tpu_custom_call" | custom-call | flops 6979321856 | bytes 27262976 | tf_op jit(solution)/shard_map/forward_send/pallas_call | solution.py:388
  67.8 59.8 %all-gather.2.cloned.1.call-done.w2g_ref = bf16[8192,896]{1,0:T(8,128)(2,1)} async-done(((bf16[128,896]{1,0:T(8,128)(2,1)}), bf16[8192,896]{1,0:T(8,128)(2,1)}) %all-gather.2.cloned.1.call-update) | async-done | bytes 14680080 | tf_op jit(solution)/shard_map/all_gather | solution.py:385
  127.6 24.2 %token_side.1.et_ref = f32[8,8192]{1,0:T(8,128)} custom-call(bf16[256,8192]{1,0:T(8,128)(2,1)} %get-tuple-element.12.u2_ref, bf16[8192,896]{1,0:T(8,128)(2,1)} %all-gather.2.cloned.1.call-done.w2g_ref, bf16[256,896]{1,0:T(8,128)(2,1)} %get-tuple-element.13.xz_ref, bf16[16,896]{1,0:T(8,128)(2,1)} %fusion.1.ht_ref, s32[8,128]{1,0:T(8,128)} %constant_dynamic-slice_fusion.lab_ref), custom_call_target="tpu_custom_call" | custom-call | flops 3489660928 | bytes 14680064 | tf_op jit(solution)/shard_map/token_side/pallas_call | solution.py:411
  151.8 4.0 %broadcast_in_dim.14.dcol_ref = f32[8,1664,128]{2,1,0:T(8,128)} broadcast(f32[8,1664]{1,0:T(8,128)S(1)} %bitcast.13), dimensions={0,1} | broadcast | bytes 6868992 | tf_op jit(solution)/shard_map/broadcast_in_dim | solution.py:426
  155.8 138.8 %task_grads.1 = (f32[8,128,1664]{2,1,0:T(8,128)}, f32[1024,1664]{1,0:T(8,128)}) custom-call(f32[8,8192]{1,0:T(8,128)} %token_side.1.et_ref, bf16[128,8192]{1,0:T(8,128)(2,1)} %get-tuple-element.14.ut_ref, f32[128,8192]{1,0:T(8,128)} %get-tuple-element.15.gpt_ref, bf16[8192,1664]{1,0:T(8,128)(2,1)} %x_ref.3, bf16[128,1664]{1,0:T(8,128)(2,1)} %w2_ref.1, ...), custom_call_target="tpu_custom_call" | custom-call | flops 83751862272 | bytes 27262976 | tf_op jit(solution)/shard_map/task_grads/pallas_call | solution.py:429
  294.6 0.0 copy-start.1
  294.6 38.8 %mix.1 = (f32[8,128]{1,0:T(8,128)}, f32[832,128]{1,0:T(8,128)}, f32[64,1664]{1,0:T(8,128)}) custom-call(f32[8,128,1664]{2,1,0:T(8,128)} %get-tuple-element.16.gdn_ref, f32[1024,1664]{1,0:T(8,128)} %get-tuple-element.17.gup_ref), custom_call_target="tpu_custom_call" | custom-call | tf_op jit(solution)/shard_map/mix/pallas_call | solution.py:450
  333.4 1.2 slice_bitcast_fusion
  334.6 1.8 copy.20
  336.4 1.8 copy.21
  338.2 0.0 copy-done.1
  (3 shorter events, 0.0 us)
Async XLA Ops:
  7.2 4.7 %copy-start = (s32[8,8192]{1,0:T(8,128)S(1)}, s32[8,8192]{1,0:T(8,128)}, u32[]{:S(2)}) copy-start(s32[8,8192]{1,0:T(8,128)} %param.9) | copy-start | bytes 786436
  7.2 120.4 %all-gather.2.cloned.1.call-start = ((), (), s32[]{:S(2)}) async-start(), calls=%async_computation | async-start | bytes 14909440 | tf_op jit(solution)/shard_map/all_gather | solution.py:385
  294.6 43.6 %copy-start.1 = (s32[8,8192]{1,0:T(8,128)S(1)}, s32[8,8192]{1,0:T(8,128)}, u32[]{:S(2)}) copy-start(s32[8,8192]{1,0:T(8,128)} %param.9) | copy-start | bytes 786436
Sparse Core Ops, SparseCore 0:
  11.4 116.0 all-gather.1

commit v2 on v1

--- a/solution.py
+++ b/solution.py
@@ -35,143 +35,249 @@
     return sem, n_model - 1 + (1 if pair else 0)
 
 
-def forward_kernel(n_model, tile, win, x_ref, w1t_ref, ut_ref, gpt_ref, u2_ref, xz_ref,
-                   xbuf, usend, xsem, send_sem, recv_sem, pair_sem):
+def forward_kernel(n_model, win, n_total, x_ref, w1t_ref, w2_ref, ht_ref, lab_ref, ut_ref, gpt_ref, et_ref,
+                   xbuf, usend, ut_s, gp_s, uslab, wslab, xz, zout, zrelay, zin, lsend, lrecv, esend,
+                   xsem, osem, usend_sem, urecv_sem, wsend_sem, wrecv_sem, psend_sem, precv_sem,
+                   zsend_sem, zrecv_sem, esend_sem, erecv_sem, lsem):
     me = lax.axis_index("model")
     core = lax.axis_index("data")
-    n_tok = x_ref.shape[0]
+    ring = 4
+    plane = ring * ring
+    n_tok, hidden = x_ref.shape
     blk = n_tok // n_model
-    n_tile = n_tok // tile
-    per = tile // blk
-    off = x_ref.shape[1] - win
+    width = w1t_ref.shape[0]
+    n_task = lab_ref.shape[0]
+    off = hidden - win
+    part = width // 2
+    px, py, pz = lax.rem(me, ring), lax.rem(lax.div(me, ring), ring), lax.div(me, plane)
+    group = lax.div(me, ring)
+    n_step = plane
+    per = plane // ring
+
+    def at(x, y, z):
+        model = lax.rem(z + ring, ring) * plane + lax.rem(y + ring, ring) * ring + lax.rem(x + ring, ring)
+        return peer(model, core)
+
+    def remote(src, dst, ssem, rsem, dev):
+        return pltpu.make_async_remote_copy(src_ref=src, dst_ref=dst, send_sem=ssem, recv_sem=rsem,
+                                            device_id=dev, device_id_type=MESH)
+
+    partner = peer(me, 1 - core)
     sem, count = ring_barrier(n_model, core, True)
-    start = lax.div(me, per)
-
-    def tile_at(i):
-        return lax.rem(i + start, n_tile)
+    shifts = (2, 1, 3, 0)
+
+    def block_of(i, k):
+        sub = lax.div(i, per)
+        shift = jnp.where(sub == 0, 2, jnp.where(sub == 1, 1, jnp.where(sub == 2, 3, 0)))
+        g = lax.rem(group + lax.rem(i, per) * per + k, plane)
+        return sub, g, g * ring + lax.rem(px + shift, ring)
 
     def fetch(i, slot):
-        rows = pl.ds(pl.multiple_of(tile_at(i) * tile, tile), tile)
-        return pltpu.make_async_copy(x_ref.at[rows, :], xbuf.at[slot], xsem.at[slot])
-
-    fetch(0, 0).start()
+        out = []
+        for k in range(per):
+            b = block_of(i, k)[2]
+            out.append(pltpu.make_async_copy(
+                x_ref.at[pl.ds(pl.multiple_of(b * blk, blk), blk), :], xbuf.at[slot, pl.ds(k * blk, blk), :],
+                xsem.at[slot, k]))
+        return out
+
+    for c in fetch(0, 0):
+        c.start()
+    w_cols = pl.ds(pl.multiple_of(core * off, LANES), win)
+    mine = pl.ds(pl.multiple_of(me * blk, blk), blk)
+    own = [pltpu.make_async_copy(x_ref.at[mine, w_cols], xz.at[0], lsem.at[0])]
+    coords = ((py, pz), (pz, py))
+    for h in range(2):
+        c1, c2 = coords[h]
+        own.append(pltpu.make_async_copy(w2_ref.at[pl.ds(h * part, part), w_cols],
+                                         wslab.at[h, c2 * ring + c1], lsem.at[1 + h]))
+    for c in own:
+        c.start()
+
+    def near(h, axis, d):
+        y_axis = (h == 0) == (axis == 0)
+        return at(px, py + d, pz) if y_axis else at(px, py, pz + d)
+
+    def gather_copy(h, stage, way):
+        c1, c2 = coords[h]
+        d = 1 if way == 0 else -1
+        sems = (wsend_sem.at[h, stage, way], wrecv_sem.at[h, stage, way])
+        if stage == 0:
+            src = w2_ref.at[pl.ds(h * part, part), w_cols]
+            return remote(src, wslab.at[h, c2 * ring + c1], *sems, near(h, 0, d))
+        if stage == 1:
+            piece = c2 * ring + lax.rem(c1 - d + ring, ring)
+            ref = wslab.at[h, piece, pl.ds(way * (part // 2), part // 2), :]
+            return remote(ref, ref, *sems, near(h, 0, d))
+        if stage == 2:
+            ref = wslab.at[h, pl.ds(c2 * ring, ring)]
+            return remote(ref, ref, *sems, near(h, 1, d))
+        ref = wslab.at[h, pl.ds(lax.rem(c2 - d + ring, ring) * ring + way * (ring // 2), ring // 2)]
+        return remote(ref, ref, *sems, near(h, 1, d))
+
+    hw = [(h, way) for h in range(2) for way in range(2)]
     pl.semaphore_wait(sem, count)
-    mine = pl.ds(pl.multiple_of(me * blk, blk), blk)
-    own_x = pltpu.make_async_copy(x_ref.at[mine, pl.ds(pl.multiple_of(core * off, LANES), win)],
-                                  xz_ref.at[pl.ds(0, blk), :], pair_sem.at[0])
-    own_x.start()
-    far_x = pltpu.make_async_remote_copy(
-        src_ref=x_ref.at[mine, pl.ds(pl.multiple_of((1 - core) * off, LANES), win)],
-        dst_ref=xz_ref.at[pl.ds(blk, blk), :], send_sem=pair_sem.at[1], recv_sem=pair_sem.at[2],
-        device_id=peer(me, 1 - core), device_id_type=MESH)
+    far_x = remote(x_ref.at[mine, pl.ds(pl.multiple_of((1 - core) * off, LANES), win)], xz.at[1],
+                   psend_sem.at[4], precv_sem.at[4], partner)
+    for h, way in hw:
+        gather_copy(h, 0, way).start()
     far_x.start()
 
     def step(i, carry):
         slot = lax.rem(i, 2)
 
-        @pl.when(i + 1 < n_tile)
+        @pl.when(i + 1 < n_step)
         def _():
-            fetch(i + 1, 1 - slot).start()
-
-        fetch(i, slot).wait()
-        base = pl.multiple_of(tile_at(i) * tile, tile)
+            for c in fetch(i + 1, 1 - slot):
+                c.start()
+
+        for c in fetch(i, slot):
+            c.wait()
         a = lax.dot_general(w1t_ref[...], xbuf[slot], NT, preferred_element_type=F32)
         a2 = a * a
         th = jnp.tanh(C_GELU * (a + K_GELU * (a * a2)))
         cdf = 0.5 * (1.0 + th)
         slope = cdf + a * (0.5 * (1.0 - th * th) * (C_GELU * (1.0 + (3.0 * K_GELU) * a2)))
         u_f = a * cdf
-        ut_ref[:, pl.ds(base, tile)] = u_f.astype(BF16)
-        gpt_ref[:, pl.ds(base, tile)] = slope
-        usend[pl.ds(base, tile), :] = u_f.T.astype(BF16)
-        dst = u2_ref.at[pl.ds(0, blk), pl.ds(pl.multiple_of(me * LANES, LANES), LANES)]
+        u_b = u_f.astype(BF16)
+        usend[pl.ds(pl.multiple_of(i * per * blk, blk), per * blk), :] = u_f.T.astype(BF16)
         for k in range(per):
-            src = usend.at[pl.ds(pl.multiple_of(base + k * blk, blk), blk), :]
-            owner = tile_at(i) * per + k
-
-            @pl.when(owner != me)
+            sub, g, b = block_of(i, k)
+            cols = pl.ds(pl.multiple_of(b * blk, blk), blk)
+            ut_s[:, cols] = u_b[:, k * blk:(k + 1) * blk]
+            gp_s[:, cols] = slope[:, k * blk:(k + 1) * blk]
+            src = usend.at[pl.ds(pl.multiple_of((i * per + k) * blk, blk), blk), :]
+            dst = uslab.at[0, sub, :, pl.ds(pl.multiple_of(group * width, width), width)]
+
+            @pl.when(g != group)
             def _():
-                pltpu.make_async_remote_copy(
-                    src_ref=src, dst_ref=dst, send_sem=send_sem, recv_sem=recv_sem,
-                    device_id=peer(owner, core), device_id_type=MESH).start()
-
-            @pl.when(owner == me)
+                remote(src, dst, usend_sem, urecv_sem.at[sub], peer(g * ring + px, core)).start()
+
+            @pl.when(g == group)
             def _():
-                pltpu.make_async_copy(src, dst, recv_sem).start()
-        return carry
-
-    lax.fori_loop(0, n_tile, step, 0)
-    own_u = u2_ref.at[pl.ds(0, blk), :]
-    pltpu.make_async_copy(own_u, own_u, recv_sem).wait()
-    far_u = pltpu.make_async_remote_copy(
-        src_ref=own_u, dst_ref=u2_ref.at[pl.ds(blk, blk), :], send_sem=pair_sem.at[3], recv_sem=pair_sem.at[4],
-        device_id=peer(me, 1 - core), device_id_type=MESH)
-    far_u.start()
-    sent = usend.at[pl.ds(0, n_tok - blk), :]
-    pltpu.make_async_copy(sent, sent, send_sem).wait()
-    own_x.wait()
-    far_x.wait()
-    far_u.wait()
-
-
-def token_kernel(n_model, chunk, n_total, u2_ref, w2g_ref, xz_ref, ht_ref, lab_ref, et_ref,
-                 wbuf, acc, lsend, lrecv, esend, wsem, pair_sem, send_sem, recv_sem):
-    me = lax.axis_index("model")
-    core = lax.axis_index("data")
-    blk = u2_ref.shape[0] // 2
-    n_chunk = w2g_ref.shape[0] // chunk
-    n_task = lab_ref.shape[0]
-    sem, count = ring_barrier(n_model, core, True)
-
-    def fetch(i, slot):
-        rows = pl.ds(pl.multiple_of(i * chunk, chunk), chunk)
-        return pltpu.make_async_copy(w2g_ref.at[rows, :], wbuf.at[slot], wsem.at[slot])
-
-    fetch(0, 0).start()
-    fetch(1, 1).start()
-    acc[...] = xz_ref[...].astype(F32) * 0.0
-
-    def step(i, carry):
-        slot = lax.rem(i, 3)
-
-        @pl.when(i + 2 < n_chunk)
-        def _():
-            fetch(i + 2, lax.rem(i + 2, 3)).start()
-
-        fetch(i, slot).wait()
-        cols = pl.ds(pl.multiple_of(i * chunk, chunk), chunk)
-        acc[...] += jnp.dot(u2_ref[:, cols], wbuf[slot], preferred_element_type=F32)
-        return carry
-
-    lax.fori_loop(0, n_chunk, step, 0)
-    z = (xz_ref[...].astype(F32) + acc[...]).astype(BF16)
-    part = lax.dot_general(ht_ref[...], z, NT, preferred_element_type=F32)
-    lsend[...] = part[:, blk:]
-    pl.semaphore_wait(sem, count)
-    swap = pltpu.make_async_remote_copy(
-        src_ref=lsend, dst_ref=lrecv, send_sem=pair_sem.at[0], recv_sem=pair_sem.at[1],
-        device_id=peer(me, 1 - core), device_id_type=MESH)
+                pltpu.make_async_copy(src, dst, urecv_sem.at[sub]).start()
+        return carry
+
+    lax.fori_loop(0, n_step // 4, step, 0)
+    for h, way in hw:
+        gather_copy(h, 0, way).wait_recv()
+        gather_copy(h, 1, way).start()
+    lax.fori_loop(n_step // 4, n_step // 2, step, 0)
+    for c in own:
+        c.wait()
+    for h, way in hw:
+        gather_copy(h, 1, way).wait_recv()
+    for h, way in hw:
+        gather_copy(h, 2, way).start()
+    lax.fori_loop(n_step // 2, n_step, step, 0)
+    out_ut = pltpu.make_async_copy(ut_s, ut_ref, osem.at[0])
+    out_gp = pltpu.make_async_copy(gp_s, gpt_ref, osem.at[1])
+    out_ut.start()
+    out_gp.start()
+    for h, way in hw:
+        gather_copy(h, 2, way).wait_recv()
+        gather_copy(h, 3, way).start()
+
+    def u_pair(s):
+        return remote(uslab.at[0, s], uslab.at[1, s], psend_sem.at[s], precv_sem.at[s], partner)
+
+    def u_arrive(s):
+        pltpu.make_async_copy(uslab.at[0, s], uslab.at[0, s], urecv_sem.at[s]).wait()
+        u_pair(s).start()
+
+    def z_copy(n):
+        left, right = at(px - 1, py, pz), at(px + 1, py, pz)
+        src, dst, dev = ((zout.at[0, 0], zrelay.at[0], right), (zout.at[0, 1], zrelay.at[1], left),
+                         (zout.at[1], zin.at[0], right), (zout.at[2], zin.at[1], left))[n]
+        return remote(src, dst, zsend_sem.at[n], zrecv_sem.at[n], dev)
+
+    def rows_of(g):
+        y, z = g % ring, g // ring
+        return [(0, z * ring + y), (1, y * ring + z)]
+
+    def partial_z(s, put):
+        for c in range(0, win, 256):
+            size = min(256, win - c)
+            total = jnp.zeros((2 * blk, size), F32)
+            for g in range(0, plane, 2):
+                left = jnp.concatenate([uslab[q, s, :, g * width:(g + 2) * width] for q in range(2)], axis=0)
+                right = jnp.concatenate([wslab[h, j, :, c:c + size] for h, j in rows_of(g) + rows_of(g + 1)], axis=0)
+                total = total + jnp.dot(left, right, preferred_element_type=F32)
+            put(c, size, total)
+
+    u_arrive(0)
+    for h, way in hw:
+        gather_copy(h, 3, way).wait_recv()
+    u_pair(0).wait_recv()
+
+    def put_far(c, size, total):
+        zout[0, 0, :, c:c + size] = total[:blk]
+        zout[0, 1, :, c:c + size] = total[blk:]
+
+    partial_z(0, put_far)
+    z_copy(0).start()
+    z_copy(1).start()
+    for s in (1, 2):
+        u_arrive(s)
+        u_pair(s).wait_recv()
+        z_copy(s - 1).wait_recv()
+
+        def put_near(c, size, total, s=s):
+            for q in range(2):
+                v = total[q * blk:(q + 1) * blk]
+                zout[s, q, :, c:c + size] = v + zrelay[q, :, c:c + size] if q == s - 1 else v
+
+        partial_z(s, put_near)
+        z_copy(s + 1).start()
+    u_arrive(3)
+    u_pair(3).wait_recv()
+    far_x.wait_recv()
+    z_copy(0).wait_send()
+    z_copy(1).wait_send()
+
+    def put_own(c, size, total):
+        for q in range(2):
+            zout[0, q, :, c:c + size] = total[q * blk:(q + 1) * blk]
+
+    partial_z(3, put_own)
+    z_copy(2).wait_recv()
+    z_copy(3).wait_recv()
+    gaps = []
+    for q in range(2):
+        z = (xz[q].astype(F32) + ((zout[0, q] + zin[0, q]) + zin[1, q])).astype(BF16)
+        gaps.append(lax.dot_general(ht_ref[...], z, NT, preferred_element_type=F32))
+    lsend[...] = gaps[1]
+    swap = remote(lsend, lrecv, psend_sem.at[5], precv_sem.at[5], partner)
     swap.start()
     swap.wait()
-    logit = part[:, :blk] + lrecv[...]
+    logit = gaps[0] + lrecv[...]
     gap = logit[:n_task, :] - logit[n_task:, :]
-    first = lab_ref[...] == 0
+    first = lab_ref[:, mine] == 0
     wrong = 1.0 / (1.0 + jnp.exp(jnp.where(first, gap, -gap)))
     esend[...] = jnp.where(first, -wrong, wrong) * (1.0 / n_total)
-
     dst = et_ref.at[:, pl.ds(pl.multiple_of(me * blk, LANES), blk)]
 
     def send(k, carry):
-        pltpu.make_async_remote_copy(
-            src_ref=esend, dst_ref=dst, send_sem=send_sem, recv_sem=recv_sem,
-            device_id=peer(lax.rem(me + k, n_model), core), device_id_type=MESH).start()
+        remote(esend, dst, esend_sem, erecv_sem, peer(lax.rem(me + k, n_model), core)).start()
         return carry
 
     lax.fori_loop(1, n_model, send, 0)
-    pltpu.make_async_copy(esend, dst, recv_sem).start()
-    pltpu.make_async_copy(et_ref, et_ref, recv_sem).wait()
+    pltpu.make_async_copy(esend, dst, erecv_sem).start()
+    for h, way in hw:
+        for stage in range(4):
+            gather_copy(h, stage, way).wait_send()
+    for s in range(4):
+        u_pair(s).wait_send()
+    far_x.wait_send()
+    z_copy(2).wait_send()
+    z_copy(3).wait_send()
+    sent = usend.at[pl.ds(0, n_tok - ring * blk), :]
+    pltpu.make_async_copy(sent, sent, usend_sem).wait()
+    out_ut.wait()
+    out_gp.wait()
+    pltpu.make_async_copy(et_ref, et_ref, erecv_sem).wait()
     sent = et_ref.at[:, pl.ds(0, (n_model - 1) * blk)]
-    pltpu.make_async_copy(sent, sent, send_sem).wait()
+    pltpu.make_async_copy(sent, sent, esend_sem).wait()
 
 
 def grad_kernel(et_ref, ut_ref, gpt_ref, x_ref, w2_ref, drow_ref, dcol_ref, gdn_ref, gup_ref,
@@ -381,46 +487,32 @@
         vmem_spec = pl.BlockSpec(memory_space=pltpu.VMEM)
         big = 60 * 1024 * 1024
 
-        w2_win = lax.dynamic_slice(w_down, (0, core * off), (width, win))
-        w2_all = lax.all_gather(w2_win, 'model', axis=0, tiled=True)
-
-        tile = min(512, n_tok)
-        ut, gpt, u2, xz = pl.pallas_call(
-            functools.partial(forward_kernel, n_model, tile, win),
-            out_shape=(jax.ShapeDtypeStruct((width, n_tok), BF16), jax.ShapeDtypeStruct((width, n_tok), F32),
-                       jax.ShapeDtypeStruct((2 * blk, n_model * width), BF16),
-                       jax.ShapeDtypeStruct((2 * blk, win), BF16)),
-            in_specs=[any_spec, vmem_spec],
-            out_specs=(vmem_spec, vmem_spec, any_spec, any_spec),
-            scratch_shapes=[pltpu.VMEM((2, tile, hidden), BF16), pltpu.VMEM((n_tok, width), BF16),
-                            pltpu.SemaphoreType.DMA((2,)), pltpu.SemaphoreType.DMA, pltpu.SemaphoreType.DMA,
-                            pltpu.SemaphoreType.DMA((5,))],
-            compiler_params=pltpu.CompilerParams(collective_id=0, has_side_effects=True, vmem_limit_bytes=big),
-            cost_estimate=pl.CostEstimate(flops=4 * n_tok * hidden * width, bytes_accessed=n_tok * hidden * 2,
-                                          transcendentals=n_tok * width),
-            name='forward_send')(tokens, w_up.T)
-
         heads = task_heads.astype(F32)
         h_t = jnp.concatenate([task_heads[:, :, 0], task_heads[:, :, 1]], axis=0)
         h_win = lax.dynamic_slice(h_t, (0, core * off), (2 * n_task, win))
         col = lax.broadcasted_iota(jnp.int32, (2 * n_task, win), 1)
         edge = core * (win - hidden // 2)
         h_win = jnp.where((col >= edge) & (col < edge + hidden // 2), h_win, jnp.zeros_like(h_win))
-        my_lab = lax.dynamic_slice(labels, (0, me * blk), (n_task, blk))
-        chunk = min(512, n_model * width)
-        e_t = pl.pallas_call(
-            functools.partial(token_kernel, n_model, chunk, n_total),
-            out_shape=jax.ShapeDtypeStruct((n_task, n_tok), F32),
-            in_specs=[vmem_spec, any_spec, vmem_spec, vmem_spec, vmem_spec],
-            out_specs=vmem_spec,
-            scratch_shapes=[pltpu.VMEM((3, chunk, win), BF16), pltpu.VMEM((2 * blk, win), F32),
+        dma = pltpu.SemaphoreType.DMA
+        e_t_shape = jax.ShapeDtypeStruct((n_task, n_tok), F32)
+        ut, gpt, e_t = pl.pallas_call(
+            functools.partial(forward_kernel, n_model, win, n_total),
+            out_shape=(jax.ShapeDtypeStruct((width, n_tok), BF16), jax.ShapeDtypeStruct((width, n_tok), F32), e_t_shape),
+            in_specs=[any_spec, vmem_spec, vmem_spec, vmem_spec, vmem_spec],
+            out_specs=(any_spec, any_spec, vmem_spec),
+            scratch_shapes=[pltpu.VMEM((2, 4 * blk, hidden), BF16), pltpu.VMEM((n_tok, width), BF16),
+                            pltpu.VMEM((width, n_tok), BF16), pltpu.VMEM((width, n_tok), F32),
+                            pltpu.VMEM((2, 4, blk, 16 * width), BF16), pltpu.VMEM((2, 16, width // 2, win), BF16),
+                            pltpu.VMEM((2, blk, win), BF16), pltpu.VMEM((3, 2, blk, win), F32),
+                            pltpu.VMEM((2, blk, win), F32), pltpu.VMEM((2, 2, blk, win), F32),
                             pltpu.VMEM((2 * n_task, blk), F32), pltpu.VMEM((2 * n_task, blk), F32),
-                            pltpu.VMEM((n_task, blk), F32), pltpu.SemaphoreType.DMA((3,)),
-                            pltpu.SemaphoreType.DMA((2,)), pltpu.SemaphoreType.DMA, pltpu.SemaphoreType.DMA],
-            compiler_params=pltpu.CompilerParams(collective_id=1, has_side_effects=True, vmem_limit_bytes=big),
-            cost_estimate=pl.CostEstimate(flops=2 * n_tok * hidden * width, bytes_accessed=n_model * width * win * 2,
-                                          transcendentals=0),
-            name='token_side')(u2, w2_all, xz, h_win, my_lab)
+                            pltpu.VMEM((n_task, blk), F32),
+                            dma((2, 4)), dma((2,)), dma, dma((4,)), dma((2, 4, 2)), dma((2, 4, 2)),
+                            dma((6,)), dma((6,)), dma((4,)), dma((4,)), dma, dma, dma((3,))],
+            compiler_params=pltpu.CompilerParams(collective_id=0, has_side_effects=True, vmem_limit_bytes=big),
+            cost_estimate=pl.CostEstimate(flops=4 * n_tok * hidden * width, bytes_accessed=n_tok * hidden * 2,
+                                          transcendentals=n_tok * width),
+            name='forward')(tokens, w_up.T, w_down, h_win, labels)
 
         d_row = heads[:, :, 0] - heads[:, :, 1]
         d_col = jnp.broadcast_to(d_row[:, :, None], (n_task, hidden, LANES))

time: 346 us -> 297 us (0.86)
  waiting for transfers between devices: 59.8 us -> 0 us
  Pallas kernels: 255 us -> 282 us
  between operations: 14.1 us -> 0.69 us
    all_gather x1 -> x0, waiting for transfers between devices: 59.8 us -> none  [local_step(): w2_all = lax.all_gather(w2_win, 'model', axis=0, tiled=True)]
    pallas_call x2 -> x1, Pallas kernels: 77.2 us -> 103 us  [local_step(): pl.pallas_call(functools.partial(forward_kernel, n_model, win, n_total),...]
  transfers between devices with their start and end apart: 1 -> 0, of which waited for: 1 -> 0; matrix products, arithmetic and copies ran while one was open for 2% -> 0% of each run, Pallas kernels for 15% -> 0%
where the time goes in v2:
time: 297 us; the launch traced here: 296 us
  Pallas kernels  282 us (95%)
  local copies, waits for them, and re-layouts  11.8 us (4%)
    pallas_call x1, Pallas kernels, local_step(): pl.pallas_call(grad_kernel, out_shape=(jax.ShapeDtypeStruct((n_task, widt...  139 us
    pallas_call x1, Pallas kernels, local_step(): pl.pallas_call(functools.partial(forward_kernel, n_model, win, n_total),...  103 us
    pallas_call x1, Pallas kernels, local_step(): pl.pallas_call(functools.partial(mix_kernel, n_model, win), out_shape=(ja...  39.9 us

profile of v2, /device:TPU:1, one launch (start us, length us, event | category | flops | bytes accessed | tf_op | source)
XLA Modules:
  0.0 296.4 jit_solution(5580184524158015938)
XLA Ops:
  0.6 0.8 convert_element_type.3
  1.5 0.7 fusion.4.drow_ref
  2.2 0.1 slice_subtract_fusion
  2.3 1.0 fusion.3
  3.3 0.6 fusion.1.ht_ref
  3.9 2.0 copy.8
  5.8 103.1 %forward.1 = (bf16[128,8192]{1,0:T(8,128)(2,1)}, f32[128,8192]{1,0:T(8,128)}, f32[8,8192]{1,0:T(8,128)}) custom-call(bf16[8192,1664]{1,0:T(8,128)(2,1)} %x_ref.3, bf16[128,1664]{1,0:T(8,128)(2,1)} %bitcast.12, bf16[128,1664]{1,0:T(8,128)(2,1)} %w2_ref.3, bf16[16,896]{1,0:T(8,128)(2,1)} %fusion.1.ht_ref, s32[8,8192]{1,0:T(8,128)} %lab_ref.1), custom_call_target="tpu_custom_call" | custom-call | flops 6979321856 | bytes 27262976 | tf_op jit(solution)/shard_map/forward/pallas_call | solution.py:498
  108.9 4.0 %broadcast_in_dim.14.dcol_ref = f32[8,1664,128]{2,1,0:T(8,128)} broadcast(f32[8,1664]{1,0:T(8,128)S(1)} %bitcast.13), dimensions={0,1} | broadcast | bytes 6868992 | tf_op jit(solution)/shard_map/broadcast_in_dim | solution.py:518
  113.0 138.8 %task_grads.1 = (f32[8,128,1664]{2,1,0:T(8,128)}, f32[1024,1664]{1,0:T(8,128)}) custom-call(f32[8,8192]{1,0:T(8,128)} %get-tuple-element.11.et_ref, bf16[128,8192]{1,0:T(8,128)(2,1)} %get-tuple-element.12.ut_ref, f32[128,8192]{1,0:T(8,128)} %get-tuple-element.13.gpt_ref, bf16[8192,1664]{1,0:T(8,128)(2,1)} %x_ref.3, bf16[128,1664]{1,0:T(8,128)(2,1)} %w2_ref.3, ...), custom_call_target="tpu_custom_call" | custom-call | flops 83751862272 | bytes 27262976 | tf_op jit(solution)/shard_map/task_grads/pallas_call | solution.py:521
  251.8 39.9 %mix.1 = (f32[8,128]{1,0:T(8,128)}, f32[832,128]{1,0:T(8,128)}, f32[64,1664]{1,0:T(8,128)}) custom-call(f32[8,128,1664]{2,1,0:T(8,128)} %get-tuple-element.14.gdn_ref, f32[1024,1664]{1,0:T(8,128)} %get-tuple-element.15.gup_ref), custom_call_target="tpu_custom_call" | custom-call | tf_op jit(solution)/shard_map/mix/pallas_call | solution.py:542
  291.6 1.2 slice_bitcast_fusion
  292.8 1.8 copy.20
  294.6 1.8 copy.21
  (3 shorter events, 0.0 us)

commit v3 on v2

--- a/solution.py
+++ b/solution.py
@@ -146,19 +146,24 @@
             cols = pl.ds(pl.multiple_of(b * blk, blk), blk)
             ut_s[:, cols] = u_b[:, k * blk:(k + 1) * blk]
             gp_s[:, cols] = slope[:, k * blk:(k + 1) * blk]
-            src = usend.at[pl.ds(pl.multiple_of((i * per + k) * blk, blk), blk), :]
-            dst = uslab.at[0, sub, :, pl.ds(pl.multiple_of(group * width, width), width)]
-
-            @pl.when(g != group)
-            def _():
-                remote(src, dst, usend_sem, urecv_sem.at[sub], peer(g * ring + px, core)).start()
-
-            @pl.when(g == group)
-            def _():
-                pltpu.make_async_copy(src, dst, urecv_sem.at[sub]).start()
+        return carry
+
+    def give(n, carry):
+        sub, g, b = block_of(lax.div(n, per), lax.rem(n, per))
+        src = usend.at[pl.ds(pl.multiple_of(n * blk, blk), blk), :]
+        dst = uslab.at[0, sub, :, pl.ds(pl.multiple_of(group * width, width), width)]
+
+        @pl.when(g != group)
+        def _():
+            remote(src, dst, usend_sem, urecv_sem.at[sub], peer(g * ring + px, core)).start()
+
+        @pl.when(g == group)
+        def _():
+            pltpu.make_async_copy(src, dst, urecv_sem.at[sub]).start()
         return carry
 
     lax.fori_loop(0, n_step // 4, step, 0)
+    lax.fori_loop(0, plane, give, 0)
     for h, way in hw:
         gather_copy(h, 0, way).wait_recv()
         gather_copy(h, 1, way).start()
@@ -177,6 +182,7 @@
     for h, way in hw:
         gather_copy(h, 2, way).wait_recv()
         gather_copy(h, 3, way).start()
+    lax.fori_loop(plane, 4 * plane, give, 0)
 
     def u_pair(s):
         return remote(uslab.at[0, s], uslab.at[1, s], psend_sem.at[s], precv_sem.at[s], partner)
@@ -280,8 +286,8 @@
     pltpu.make_async_copy(sent, sent, esend_sem).wait()
 
 
-def grad_kernel(et_ref, ut_ref, gpt_ref, x_ref, w2_ref, drow_ref, dcol_ref, gdn_ref, gup_ref,
-                dn_acc, up_acc, ebr, dat, out_sem):
+def grad_kernel(et_ref, ut_ref, gpt_ref, x_ref, w2_ref, drow_ref, gdn_ref, gup_ref,
+                dn_acc, up_acc, dcol, ebr, dat, out_sem):
     step = pl.program_id(0)
     n_task, tile = et_ref.shape
     width, hidden = w2_ref.shape
@@ -293,39 +299,44 @@
         dn_acc[...] = jnp.zeros_like(dn_acc)
         up_acc[...] = jnp.zeros_like(up_acc)
 
+        def spread(t, carry):
+            dcol[t] = jnp.broadcast_to(drow_ref[t], (LANES, hidden)).T
+            return carry
+
+        lax.fori_loop(0, n_task, spread, 0)
+
     for t in range(n_task):
         ebr[t] = et_ref[t:t + 1, :]
 
-    def one_task(t, carry):
-        e_row = ebr[t]
-        for n in range(0, tile, wide):
-            e_n = e_row[:, n:n + wide]
-            da = jnp.zeros((width, wide), F32)
+    def pair_of_tasks(m, carry):
+        rows = pl.ds(pl.multiple_of(2 * m * width, 2 * width), 2 * width)
+        e_cols = []
+        for q in range(2):
+            t = 2 * m + q
+            e_row = ebr[t]
+            for n in range(0, tile, wide):
+                e_n = e_row[:, n:n + wide]
+                da = jnp.zeros((width, wide), F32)
+                for c, size in cuts:
+                    d_c = dcol[t, c:c + size, :]
+                    d_c = jnp.concatenate([d_c] * (wide // LANES), axis=1)
+                    dz_t = (d_c * e_n).astype(BF16)
+                    da = da + jnp.dot(w2_ref[:, c:c + size], dz_t, preferred_element_type=F32)
+                dat[pl.ds(pl.multiple_of(t * width, width), width), n:n + wide] = (
+                    da * gpt_ref[:, n:n + wide]).astype(BF16)
+        for q in range(2):
+            t = 2 * m + q
+            e_col = jnp.broadcast_to(ebr[t], (LANES, tile)).T
             for c, size in cuts:
-                d_c = dcol_ref[t, c:c + size, :]
-                d_c = jnp.concatenate([d_c] * (wide // LANES), axis=1)
-                dz_t = (d_c * e_n).astype(BF16)
-                da = da + jnp.dot(w2_ref[:, c:c + size], dz_t, preferred_element_type=F32)
-            dat[pl.ds(pl.multiple_of(t * width, width), width), n:n + wide] = (da * gpt_ref[:, n:n + wide]).astype(BF16)
-        e_col = jnp.broadcast_to(e_row, (LANES, tile)).T
+                e_b = jnp.concatenate([e_col] * (size // LANES), axis=1)
+                dz = (e_b * drow_ref[t, :, c:c + size]).astype(BF16)
+                dn_acc[t, :, c:c + size] += jnp.dot(ut_ref[...], dz, preferred_element_type=F32)
+        left = dat[rows, :]
         for c, size in cuts:
-            e_b = e_col
-            e_b = jnp.concatenate([e_b] * (size // LANES), axis=1)
-            dz = (e_b * drow_ref[t, :, c:c + size]).astype(BF16)
-            dn_acc[t, :, c:c + size] += jnp.dot(ut_ref[...], dz, preferred_element_type=F32)
-        return carry
-
-    lax.fori_loop(0, n_task, one_task, 0)
-    rows = 2 * width
-
-    def up_part(m, carry):
-        at = pl.ds(pl.multiple_of(m * rows, rows), rows)
-        left = dat[at, :]
-        for c, size in cuts:
-            up_acc[at, c:c + size] += jnp.dot(left, x_ref[:, c:c + size], preferred_element_type=F32)
-        return carry
-
-    lax.fori_loop(0, n_task * width // rows, up_part, 0)
+            up_acc[rows, c:c + size] += jnp.dot(left, x_ref[:, c:c + size], preferred_element_type=F32)
+        return carry
+
+    lax.fori_loop(0, n_task // 2, pair_of_tasks, 0)
 
     @pl.when(step == pl.num_programs(0) - 1)
     def _():
@@ -515,8 +526,7 @@
             name='forward')(tokens, w_up.T, w_down, h_win, labels)
 
         d_row = heads[:, :, 0] - heads[:, :, 1]
-        d_col = jnp.broadcast_to(d_row[:, :, None], (n_task, hidden, LANES))
-        t_b = min(512, n_tok)
+        t_b = min(1024, n_tok)
         const2 = lambda i: (0, 0)
         g_dn, g_up = pl.pallas_call(
             grad_kernel,
@@ -526,17 +536,16 @@
             in_specs=[pl.BlockSpec((n_task, t_b), lambda i: (0, i)), pl.BlockSpec((width, t_b), lambda i: (0, i)),
                       pl.BlockSpec((width, t_b), lambda i: (0, i)), pl.BlockSpec((t_b, hidden), lambda i: (i, 0)),
                       pl.BlockSpec((width, hidden), const2, pipeline_mode=pl.Buffered(1)),
-                      pl.BlockSpec((n_task, 1, hidden), lambda i: (0, 0, 0), pipeline_mode=pl.Buffered(1)),
-                      pl.BlockSpec((n_task, hidden, LANES), lambda i: (0, 0, 0), pipeline_mode=pl.Buffered(1))],
+                      pl.BlockSpec((n_task, 1, hidden), lambda i: (0, 0, 0), pipeline_mode=pl.Buffered(1))],
             out_specs=(any_spec, any_spec),
             scratch_shapes=[pltpu.VMEM((n_task, width, hidden), F32), pltpu.VMEM((n_task * width, hidden), F32),
-                            pltpu.VMEM((n_task, 1, t_b), F32),
+                            pltpu.VMEM((n_task, hidden, LANES), F32), pltpu.VMEM((n_task, 1, t_b), F32),
                             pltpu.VMEM((n_task * width, t_b), BF16),
                             pltpu.SemaphoreType.DMA((2,))],
             compiler_params=pltpu.CompilerParams(dimension_semantics=('arbitrary',), vmem_limit_bytes=big),
             cost_estimate=pl.CostEstimate(flops=48 * n_tok * hidden * width, bytes_accessed=n_tok * hidden * 2,
                                           transcendentals=0),
-            name='task_grads')(e_t, ut, gpt, tokens, w_down, d_row[:, None, :], d_col)
+            name='task_grads')(e_t, ut, gpt, tokens, w_down, d_row[:, None, :])
 
         half = width // 2
         weights, grad_up, grad_down = pl.pallas_call(

time: 297 us -> 272 us (0.916)
  Pallas kernels: 282 us -> 261 us
  local copies, waits for them, and re-layouts: 11.8 us -> 7.73 us
    pallas_call x1, Pallas kernels: 139 us -> 118 us  [local_step(): pl.pallas_call(grad_kernel, out_shape=(jax.ShapeDtypeStruct((n_task, widt...]
    broadcast_in_dim x1 -> x0, local copies, waits for them, and re-layouts: 4.03 us -> none  [local_step(): d_col = jnp.broadcast_to(d_row[:, :, None], (n_task, hidden, LANES))]
where the time goes in v3:
time: 272 us
  Pallas kernels  261 us (96%)
  local copies, waits for them, and re-layouts  7.73 us (3%)
    pallas_call x1, Pallas kernels, local_step(): pl.pallas_call(grad_kernel, out_shape=(jax.ShapeDtypeStruct((n_task, widt...  118 us
    pallas_call x1, Pallas kernels, local_step(): pl.pallas_call(functools.partial(forward_kernel, n_model, win, n_total),...  103 us
    pallas_call x1, Pallas kernels, local_step(): pl.pallas_call(functools.partial(mix_kernel, n_model, win), out_shape=(ja...  40.2 us
    unnamed x3, local copies, waits for them, and re-layouts  5.55 us

profile of v3, /device:TPU:1, one launch (start us, length us, event | category | flops | bytes accessed | tf_op | source)
XLA Modules:
  0.0 271.7 jit_solution(12135851300184197428)
XLA Ops:
  0.6 0.8 convert_element_type.3
  1.5 0.7 fusion.drow_ref
  2.2 1.0 fusion.4
  3.2 0.6 fusion.2.ht_ref
  3.8 2.0 copy.8
  5.8 103.3 %forward.1 = (bf16[128,8192]{1,0:T(8,128)(2,1)}, f32[128,8192]{1,0:T(8,128)}, f32[8,8192]{1,0:T(8,128)}) custom-call(bf16[8192,1664]{1,0:T(8,128)(2,1)} %x_ref.3, bf16[128,1664]{1,0:T(8,128)(2,1)} %bitcast.9, bf16[128,1664]{1,0:T(8,128)(2,1)} %w2_ref.3, bf16[16,896]{1,0:T(8,128)(2,1)} %fusion.2.ht_ref, s32[8,8192]{1,0:T(8,128)} %lab_ref.1), custom_call_target="tpu_custom_call" | custom-call | flops 6979321856 | bytes 27262976 | tf_op jit(solution)/shard_map/forward/pallas_call | solution.py:509
  109.1 117.6 %task_grads.1 = (f32[8,128,1664]{2,1,0:T(8,128)}, f32[1024,1664]{1,0:T(8,128)}) custom-call(f32[8,8192]{1,0:T(8,128)} %get-tuple-element.11.et_ref, bf16[128,8192]{1,0:T(8,128)(2,1)} %get-tuple-element.12.ut_ref, f32[128,8192]{1,0:T(8,128)} %get-tuple-element.13.gpt_ref, bf16[8192,1664]{1,0:T(8,128)(2,1)} %x_ref.3, bf16[128,1664]{1,0:T(8,128)(2,1)} %w2_ref.3, ...), custom_call_target="tpu_custom_call" | custom-call | flops 83751862272 | bytes 27262976 | tf_op jit(solution)/shard_map/task_grads/pallas_call | solution.py:531
  226.7 40.2 %mix.1 = (f32[8,128]{1,0:T(8,128)}, f32[832,128]{1,0:T(8,128)}, f32[64,1664]{1,0:T(8,128)}) custom-call(f32[8,128,1664]{2,1,0:T(8,128)} %get-tuple-element.14.gdn_ref, f32[1024,1664]{1,0:T(8,128)} %get-tuple-element.15.gup_ref), custom_call_target="tpu_custom_call" | custom-call | tf_op jit(solution)/shard_map/mix/pallas_call | solution.py:551
  266.9 1.2 slice_bitcast_fusion
  268.1 1.8 copy.17
  269.9 1.8 copy.18
  (2 shorter events, 0.0 us)

commit v4 on v0

v4 whole, which is shorter than its diff:
```python
import functools

import jax
import jax.numpy as jnp
from jax import lax
from jax.experimental import pallas as pl
from jax.experimental.pallas import tpu as pltpu
from jax.sharding import PartitionSpec as P

STEPS = 20
LANES = 128
MESH = pl.DeviceIdType.MESH
F32 = jnp.float32
BF16 = jnp.bfloat16
C_GELU = 0.7978845608028654
K_GELU = 0.044715
NT = (((1,), (1,)), ((), ()))


def peer(model, data):
    return {"model": model, "data": data}


def step_kernel(n_model, win, n_total, x_ref, w1t_ref, w2_ref, ht_ref, lab_ref, drow_ref, a_ref, g1_ref, g2_ref,
                xbuf, usend, ut_s, gp_s, uslab, wslab, xz, zall, lsend, lrecv, esend, et,
                dn_acc, up_acc, dcol, ebr, dat, msend, mrecv, g1t,
                xsem, usend_sem, urecv_sem, wsend_sem, wrecv_sem, psend_sem, precv_sem, zsend_sem, zrecv_sem,
                esend_sem, erecv_sem, lsem, gsend_sem, grecv_sem, msend_sem, mrecv_sem, free_sem):
    me = lax.axis_index("model")
    core = lax.axis_index("data")
    ring = 4
    plane = ring * ring
    n_tok, hidden = x_ref.shape
    blk = n_tok // n_model
    sub_blk = blk // 2
    width = w1t_ref.shape[0]
    half = width // 2
    n_task = lab_ref.shape[0]
    off = hidden - win
    tile = plane * sub_blk
    n_tile = 2 * ring
    n_all = 2 * n_model
    slot_of_me = me * 2 + core
    px, py, pz = lax.rem(me, ring), lax.rem(lax.div(me, ring), ring), lax.div(me, plane)
    group = lax.div(me, ring)
    partner = peer(me, 1 - core)
    wide = 256
    cuts = [(c, min(wide, hidden - c)) for c in range(0, hidden, wide)]

    def at(x, y, z):
        model = lax.rem(z + ring, ring) * plane + lax.rem(y + ring, ring) * ring + lax.rem(x + ring, ring)
        return peer(model, core)

    def remote(src, dst, ssem, rsem, dev):
        return pltpu.make_async_remote_copy(src_ref=src, dst_ref=dst, send_sem=ssem, recv_sem=rsem,
                                            device_id=dev, device_id_type=MESH)

    def other(k):
        dev = lax.rem(slot_of_me + k, n_all)
        return peer(lax.div(dev, 2), lax.rem(dev, 2))

    sem = pltpu.get_barrier_semaphore()

    def tell(k, carry):
        pl.semaphore_signal(sem, inc=1, device_id=other(k), device_id_type=MESH)
        return carry

    lax.fori_loop(1, n_all, tell, 0)

    def block_of(j, k):
        sub = lax.rem(j, ring)
        shift = jnp.where(sub == 0, 2, jnp.where(sub == 1, 1, jnp.where(sub == 2, 3, 0)))
        return lax.rem(group + k, plane) * ring + lax.rem(px + shift, ring)

    def fetch(j, slot):
        def one(k, carry):
            row = block_of(j, k) * blk + lax.div(j, ring) * sub_blk
            pltpu.make_async_copy(x_ref.at[pl.ds(pl.multiple_of(row, sub_blk), sub_blk), :],
                                  xbuf.at[slot, pl.ds(pl.multiple_of(k * sub_blk, sub_blk), sub_blk), :],
                                  xsem.at[slot]).start()
            return carry

        lax.fori_loop(0, plane, one, 0)

    def fetched(slot):
        pltpu.make_async_copy(xbuf.at[slot], xbuf.at[slot], xsem.at[slot]).wait()

    fetch(0, 0)
    w_cols = pl.ds(pl.multiple_of(core * off, LANES), win)
    far_cols = pl.ds(pl.multiple_of((1 - core) * off, LANES), win)
    mine = pl.ds(pl.multiple_of(me * blk, blk), blk)
    own = [pltpu.make_async_copy(x_ref.at[mine, w_cols], xz.at[0], lsem.at[0])]
    coords = ((py, pz), (pz, py))
    for h in range(2):
        c1, c2 = coords[h]
        own.append(pltpu.make_async_copy(w2_ref.at[pl.ds(h * half, half), w_cols],
                                         wslab.at[h, c2 * ring + c1], lsem.at[1 + h]))
    for c in own:
        c.start()

    def near(h, axis, d):
        y_axis = (h == 0) == (axis == 0)
        return at(px, py + d, pz) if y_axis else at(px, py, pz + d)

    def gather_copy(h, stage, way):
        c1, c2 = coords[h]
        d = 1 if way == 0 else -1
        sems = (wsend_sem.at[h, stage, way], wrecv_sem.at[h, stage, way])
        if stage == 0:
            src = w2_ref.at[pl.ds(h * half, half), w_cols]
            return remote(src, wslab.at[h, c2 * ring + c1], *sems, near(h, 0, d))
        if stage == 1:
            piece = c2 * ring + lax.rem(c1 - d + ring, ring)
            ref = wslab.at[h, piece, pl.ds(way * (half // 2), half // 2), :]
            return remote(ref, ref, *sems, near(h, 0, d))
        if stage == 2:
            ref = wslab.at[h, pl.ds(c2 * ring, ring)]
            return remote(ref, ref, *sems, near(h, 1, d))
        ref = wslab.at[h, pl.ds(lax.rem(c2 - d + ring, ring) * ring + way * (ring // 2), ring // 2)]
        return remote(ref, ref, *sems, near(h, 1, d))

    hw = [(h, way) for h in range(2) for way in range(2)]
    dn_acc[...] = jnp.zeros_like(dn_acc)
    up_acc[...] = jnp.zeros_like(up_acc)

    def spread(t, carry):
        dcol[t] = jnp.broadcast_to(drow_ref[t], (LANES, hidden)).T
        return carry

    lax.fori_loop(0, n_task, spread, 0)
    pl.semaphore_wait(sem, n_all - 1)
    far_x = remote(x_ref.at[mine, far_cols], xz.at[1], psend_sem.at[2, 0], precv_sem.at[2, 0], partner)
    for h, way in hw:
        gather_copy(h, 0, way).start()
    far_x.start()

    def forward(j, carry):
        slot = lax.rem(j, 2)

        @pl.when(j + 1 < n_tile)
        def _():
            fetch(j + 1, 1 - slot)

        fetched(slot)
        base = pl.multiple_of(j * tile, tile)
        step = min(512, tile)
        for n in range(0, tile, step):
            a = lax.dot_general(w1t_ref[...], xbuf[slot, n:n + step, :], NT, preferred_element_type=F32)
            a2 = a * a
            th = jnp.tanh(C_GELU * (a + K_GELU * (a * a2)))
            cdf = 0.5 * (1.0 + th)
            slope = cdf + a * (0.5 * (1.0 - th * th) * (C_GELU * (1.0 + (3.0 * K_GELU) * a2)))
            u_f = a * cdf
            ut_s[:, pl.ds(pl.multiple_of(base + n, step), step)] = u_f.astype(BF16)
            gp_s[:, pl.ds(pl.multiple_of(base + n, step), step)] = slope
            usend[pl.ds(pl.multiple_of(base + n, step), step), :] = u_f.T.astype(BF16)
        return carry

    def give(n, carry):
        j = lax.div(n, plane)
        k = lax.rem(n, plane)
        part, sub = lax.div(j, ring), lax.rem(j, ring)
        g = lax.rem(group + k, plane)
        src = usend.at[pl.ds(pl.multiple_of(n * sub_blk, sub_blk), sub_blk), :]
        dst = uslab.at[part, 0, sub, :, pl.ds(pl.multiple_of(group * width, width), width)]

        @pl.when(g != group)
        def _():
            remote(src, dst, usend_sem, urecv_sem.at[part, sub], peer(g * ring + px, core)).start()

        @pl.when(g == group)
        def _():
            pltpu.make_async_copy(src, dst, urecv_sem.at[part, sub]).start()
        return carry

    lax.fori_loop(0, 1, forward, 0)
    lax.fori_loop(0, plane, give, 0)
    for h, way in hw:
        gather_copy(h, 0, way).wait_recv()
        gather_copy(h, 1, way).start()
    lax.fori_loop(1, 2, forward, 0)
    for c in own:
        c.wait()
    for h, way in hw:
        gather_copy(h, 1, way).wait_recv()
    for h, way in hw:
        gather_copy(h, 2, way).start()
    lax.fori_loop(2, n_tile, forward, 0)
    fetch(0, 0)
    for h, way in hw:
        gather_copy(h, 2, way).wait_recv()
        gather_copy(h, 3, way).start()
    lax.fori_loop(plane, ring * plane, give, 0)

    def u_pair(part, s):
        return remote(uslab.at[part, 0, s], uslab.at[part, 1, s], psend_sem.at[part, s], precv_sem.at[part, s], partner)

    def u_arrive(part, s):
        ref = uslab.at[part, 0, s]
        pltpu.make_async_copy(ref, ref, urecv_sem.at[part, s]).wait()
        u_pair(part, s).start()

    def z_out(part, n, q):
        return part * 6 + n * 2 + q

    def z_relay(part, q):
        return 12 + part * 2 + q

    def z_in(part, i, q):
        return 16 + part * 4 + i * 2 + q

    def z_copy(part, n):
        left, right = at(px - 1, py, pz), at(px + 1, py, pz)
        src, dst, dev = ((zall.at[z_out(part, 0, 0)], zall.at[z_relay(part, 0)], right),
                         (zall.at[z_out(part, 0, 1)], zall.at[z_relay(part, 1)], left),
                         (zall.at[pl.ds(z_out(part, 1, 0), 2)], zall.at[pl.ds(z_in(part, 0, 0), 2)], right),
                         (zall.at[pl.ds(z_out(part, 2, 0), 2)], zall.at[pl.ds(z_in(part, 1, 0), 2)], left))[n]
        return remote(src, dst, zsend_sem.at[part, n], zrecv_sem.at[part, n], dev)

    def rows_of(g):
        y, z = g % ring, g // ring
        return [(0, z * ring + y), (1, y * ring + z)]

    def partial_z(part, s, put):
        for c in range(0, win, wide):
            size = min(wide, win - c)
            total = jnp.zeros((2 * sub_blk, size), F32)
            for g in range(0, plane, 2):
                left = jnp.concatenate(
                    [uslab[part, q, s, :, g * width:(g + 2) * width] for q in range(2)], axis=0)
                right = jnp.concatenate([wslab[h, i, :, c:c + size] for h, i in rows_of(g) + rows_of(g + 1)], axis=0)
                total = total + jnp.dot(left, right, preferred_element_type=F32)
            put(c, size, total[:sub_blk], total[sub_blk:])

    def z_far(part):
        u_pair(part, 0).wait_recv()

        def put(c, size, top, low):
            zall[z_out(part, 0, 0), :, c:c + size] = top
            zall[z_out(part, 0, 1), :, c:c + size] = low

        partial_z(part, 0, put)
        z_copy(part, 0).start()
        z_copy(part, 1).start()

    def z_near(part, s):
        u_pair(part, s).wait_recv()
        z_copy(part, s - 1).wait_recv()

        def put(c, size, top, low):
            for q, v in enumerate((top, low)):
                if q == s - 1:
                    v = v + zall[z_relay(part, q), :, c:c + size]
                zall[z_out(part, s, q), :, c:c + size] = v

        partial_z(part, s, put)
        z_copy(part, s + 1).start()

    def z_own(part):
        u_pair(part, 3).wait_recv()
        z_copy(part, 0).wait_send()
        z_copy(part, 1).wait_send()

        def put(c, size, top, low):
            zall[z_out(part, 0, 0), :, c:c + size] = top
            zall[z_out(part, 0, 1), :, c:c + size] = low

        partial_z(part, 3, put)

    pad = jnp.zeros((n_task, LANES - sub_blk), F32)

    def e_out(part):
        z_copy(part, 2).wait_recv()
        z_copy(part, 3).wait_recv()
        z_copy(part, 2).wait_send()
        z_copy(part, 3).wait_send()
        gaps = []
        rows = slice(part * sub_blk, (part + 1) * sub_blk)
        for q in range(2):
            z = (xz[q, rows, :].astype(F32) + ((zall[z_out(part, 0, q)] + zall[z_in(part, 0, q)]) + zall[z_in(part, 1, q)])).astype(BF16)
            gaps.append(lax.dot_general(ht_ref[...], z, NT, preferred_element_type=F32))
        lsend[part] = jnp.concatenate([gaps[1], jnp.concatenate([pad, pad], axis=0)], axis=1)
        swap = remote(lsend.at[part], lrecv.at[part], psend_sem.at[2, 1 + part], precv_sem.at[2, 1 + part], partner)
        swap.start()
        swap.wait()
        logit = gaps[0] + lrecv[part, :, :sub_blk]
        gap = logit[:n_task, :] - logit[n_task:, :]
        first = lab_ref[:, mine][:, rows] == 0
        wrong = 1.0 / (1.0 + jnp.exp(jnp.where(first, gap, -gap)))
        e = jnp.where(first, -wrong, wrong) * (1.0 / n_total)
        esend[part] = jnp.concatenate([e, pad], axis=1)
        dst = et.at[part, me]

        def send(k, carry):
            remote(esend.at[part], dst, esend_sem.at[part], erecv_sem.at[part],
                   peer(lax.rem(me + k, n_model), core)).start()
            return carry

        lax.fori_loop(1, n_model, send, 0)
        pltpu.make_async_copy(esend.at[part], dst, erecv_sem.at[part]).start()

    def e_in(part):
        pltpu.make_async_copy(et.at[part], et.at[part], erecv_sem.at[part]).wait()

    u_arrive(0, 0)
    for h, way in hw:
        gather_copy(h, 3, way).wait_recv()
    z_far(0)
    u_arrive(0, 1)
    z_near(0, 1)
    u_arrive(0, 2)
    z_near(0, 2)
    u_arrive(0, 3)
    lax.fori_loop(ring * plane, n_tile * plane, give, 0)
    far_x.wait_recv()
    z_own(0)
    e_out(0)
    e_in(0)

    def far_down(t):
        rows = pl.ds(pl.multiple_of(lax.rem(t, 2) * half, half), half)
        return gp_s.at[rows, pl.ds(pl.multiple_of(lax.div(t, 2) * hidden, LANES), hidden)]

    def grad_copies(t):
        out = [remote(dn_acc.at[t, pl.ds(pl.multiple_of((1 - core) * half, half), half), :], far_down(t),
                      gsend_sem.at[0, t], grecv_sem.at[0, t], partner)]
        for i in range(2):
            rows = pl.ds(pl.multiple_of(t * width + i * half, half), half)
            out.append(remote(up_acc.at[rows, far_cols], zall.at[2 * t + i],
                              gsend_sem.at[1 + i, t], grecv_sem.at[1 + i, t], partner))
        return out

    def grad_tile(j, carry):
        slot = lax.rem(j, 2)

        @pl.when(j + 1 < n_tile)
        def _():
            fetch(j + 1, 1 - slot)

        @pl.when(j == n_tile - 1)
        def _():
            pl.semaphore_signal(free_sem, inc=1, device_id=partner, device_id_type=MESH)

        part = lax.div(j, ring)
        for k in range(0, plane, 2):
            pieces = [et[part, block_of(j, k + i)][:, :sub_blk] for i in range(2)]
            e_pair = jnp.concatenate(pieces, axis=1)
            for t in range(n_task):
                ebr[t, :, k * sub_blk:(k + 2) * sub_blk] = e_pair[t:t + 1, :]
        fetched(slot)
        base = pl.multiple_of(j * tile, tile)

        def pair_of_tasks(m, carry):
            rows = pl.ds(pl.multiple_of(2 * m * width, 2 * width), 2 * width)
            for q in range(2):
                t = 2 * m + q
                for n in range(0, tile, wide):
                    n_size = min(wide, tile)
                    e_n = ebr[t, :, n:n + n_size]
                    da = jnp.zeros((width, n_size), F32)
                    for c, size in cuts:
                        d_c = jnp.concatenate([dcol[t, c:c + size, :]] * (n_size // LANES), axis=1)
                        dz_t = (d_c * e_n).astype(BF16)
                        da = da + jnp.dot(w2_ref[:, c:c + size], dz_t, preferred_element_type=F32)
                    cols = pl.ds(pl.multiple_of(base + n, n_size), n_size)
                    dat[q * width:(q + 1) * width, n:n + n_size] = (da * gp_s[:, cols]).astype(BF16)
            for q in range(2):
                t = 2 * m + q
                e_col = jnp.broadcast_to(ebr[t], (LANES, tile)).T
                for c, size in cuts:
                    e_b = jnp.concatenate([e_col] * (size // LANES), axis=1)
                    dz = (e_b * drow_ref[t, :, c:c + size]).astype(BF16)
                    dn_acc[t, :, c:c + size] += jnp.dot(ut_s[:, pl.ds(base, tile)], dz, preferred_element_type=F32)
            left = dat[...]
            for c, size in cuts:
                up_acc[rows, c:c + size] += jnp.dot(left, xbuf[slot, :, c:c + size], preferred_element_type=F32)

            @pl.when((j == n_tile - 1) & (m == 0))
            def _():
                pl.semaphore_wait(free_sem, 1)

            @pl.when(j == n_tile - 1)
            def _():
                for q in range(2):
                    for c in grad_copies(2 * m + q):
                        c.start()
            return carry

        lax.fori_loop(0, n_task // 2, pair_of_tasks, 0)

        @pl.when(j == 0)
        def _():
            for s in range(4):
                u_arrive(1, s)
            z_far(1)

        @pl.when(j == 1)
        def _():
            z_near(1, 1)
            z_near(1, 2)
            z_own(1)

        @pl.when(j == 2)
        def _():
            e_out(1)

        @pl.when(j == 3)
        def _():
            e_in(1)
        return carry

    lax.fori_loop(0, n_tile, grad_tile, 0)

    def landed(t, carry):
        for c in grad_copies(t):
            c.wait_recv()
        return carry

    lax.fori_loop(0, n_task, landed, 0)
    pairs = [(t, s) for t in range(n_task) for s in range(t, n_task)]
    lane = lax.broadcasted_iota(jnp.int32, (8, LANES), 1)

    def gram_of(vals, sums):
        return tuple(acc + vals[t] * vals[s] for acc, (t, s) in zip(sums, pairs))

    def down_at(t, r, c):
        return (pl.ds(pl.multiple_of((t % 2) * half + r * 8, 8), 8), slice((t // 2) * hidden + c, (t // 2) * hidden + c + LANES))

    def fold_down(r, sums):
        from_acc = pl.ds(pl.multiple_of(core * half + r * 8, 8), 8)
        for c in range(0, hidden, LANES):
            vals = []
            for t in range(n_task):
                v = dn_acc[t, from_acc, c:c + LANES] + gp_s[down_at(t, r, c)]
                gp_s[down_at(t, r, c)] = v
                vals.append(v)
            sums = gram_of(vals, sums)
        return sums

    first = core * (win - hidden // 2)

    def fold_up(i, r, sums):
        rows = pl.ds(pl.multiple_of(r * 8, 8), 8)
        for c in range(0, win, LANES):
            edge = c < win - hidden // 2 or c + LANES > hidden // 2
            vals = []
            for t in range(n_task):
                v = up_acc[pl.ds(pl.multiple_of(t * width + i * half + r * 8, 8), 8),
                           pl.ds(pl.multiple_of(core * off + c, LANES), LANES)] + zall[2 * t + i, rows, c:c + LANES]
                zall[2 * t + i, rows, c:c + LANES] = v
                vals.append(jnp.where((lane + c >= first) & (lane + c < first + hidden // 2), v, 0.0) if edge else v)
            sums = gram_of(vals, sums)
        return sums

    sums = tuple(jnp.zeros((8, LANES), F32) for _ in pairs)
    sums = lax.fori_loop(0, half // 8, fold_down, sums)
    for i in range(2):
        sums = lax.fori_loop(0, half // 8, functools.partial(fold_up, i), sums)
    lane1 = lax.broadcasted_iota(jnp.int32, (1, LANES), 1)
    row = lax.broadcasted_iota(jnp.int32, (8, LANES), 0)
    out = jnp.zeros((1, LANES), F32)
    for acc, (t, s) in zip(sums, pairs):
        total = jnp.sum(jnp.sum(acc, axis=0, keepdims=True), axis=1, keepdims=True)
        out = out + jnp.where((lane1 == t * n_task + s) | (lane1 == s * n_task + t), total, 0.0)
    msend[...] = out

    def send_gram(k, carry):
        remote(msend, mrecv.at[slot_of_me], msend_sem, mrecv_sem, other(k)).start()
        return carry

    lax.fori_loop(1, n_all, send_gram, 0)
    pltpu.make_async_copy(msend, mrecv.at[slot_of_me], mrecv_sem).start()
    pltpu.make_async_copy(mrecv, mrecv, mrecv_sem).wait()
    flat = jnp.sum(mrecv[...], axis=0)
    gram = jnp.zeros((8, LANES), F32)
    for t in range(n_task):
        line = flat if t == 0 else pltpu.roll(flat, LANES - t * n_task, 1)
        gram = gram + jnp.where((row == t) & (lane < n_task), jnp.broadcast_to(line, (8, LANES)), 0.0)
    scale = jnp.sum(jnp.sum(jnp.where(row == lane, gram, 0.0), axis=1, keepdims=True), axis=0, keepdims=True) / n_task
    gram = gram / scale
    w = jnp.where(lane < n_task, 1.0 / n_task, 0.0).astype(F32)

    def eg_pair(i, w):
        v = jnp.sum(gram * w, axis=1, keepdims=True)
        w_col = jnp.sum(jnp.where(row == lane, w, 0.0), axis=1, keepdims=True)
        w_col = w_col * jnp.exp(-v)
        w_col = w_col / jnp.sum(w_col, axis=0, keepdims=True)
        v = jnp.sum(gram * w_col, axis=0, keepdims=True)
        w_row = jnp.sum(jnp.where(row == lane, w_col, 0.0), axis=0, keepdims=True)
        w_row = w_row * jnp.exp(-v)
        w_row = w_row / jnp.sum(w_row, axis=1, keepdims=True)
        return jnp.broadcast_to(w_row, (8, LANES))

    w = lax.fori_loop(0, STEPS // 2, eg_pair, w)
    a_ref[...] = w
    a = [jnp.broadcast_to(jnp.sum(jnp.where(lane == t, w, 0.0), axis=1, keepdims=True), (8, LANES))
         for t in range(n_task)]

    def mix_down(r, carry):
        rows = pl.ds(pl.multiple_of(r * 8, 8), 8)
        for c in range(0, hidden, LANES):
            total = a[0] * gp_s[down_at(0, r, c)]
            for t in range(1, n_task):
                total = total + a[t] * gp_s[down_at(t, r, c)]
            g2_ref[rows, c:c + LANES] = total
        return carry

    last = z_in(0, 0, 0)

    def mix_up(i, r, carry):
        rows = pl.ds(pl.multiple_of(r * 8, 8), 8)
        for c in range(0, win, LANES):
            total = a[0] * zall[i, rows, c:c + LANES]
            for t in range(1, n_task):
                total = total + a[t] * zall[2 * t + i, rows, c:c + LANES]
            zall[last + i, rows, c:c + LANES] = total
        return carry

    lax.fori_loop(0, half // 8, mix_down, 0)
    for i in range(2):
        lax.fori_loop(0, half // 8, functools.partial(mix_up, i), 0)
    for c in range(0, win, LANES):
        g1t[c:c + LANES, :] = jnp.concatenate([zall[last + i, :, c:c + LANES] for i in range(2)], axis=0).T
    g1_ref[...] = g1t[pl.ds(pl.multiple_of(first, 8), hidden // 2), :]

    for h, way in hw:
        for stage in range(4):
            gather_copy(h, stage, way).wait_send()
    for part in range(2):
        for s in range(4):
            u_pair(part, s).wait_send()
        sent = et.at[part, pl.ds(0, n_model - 1)]
        pltpu.make_async_copy(sent, sent, esend_sem.at[part]).wait()
    far_x.wait_send()
    sent = usend.at[pl.ds(0, n_tok - ring * blk), :]
    pltpu.make_async_copy(sent, sent, usend_sem).wait()

    def gone(t, carry):
        for c in grad_copies(t):
            c.wait_send()
        return carry

    lax.fori_loop(0, n_task, gone, 0)
    sent = mrecv.at[pl.ds(0, n_all - 1)]
    pltpu.make_async_copy(sent, sent, msend_sem).wait()


def solution(mesh):
    n_model, n_data = mesh.shape['model'], mesh.shape['data']

    def local_step(tokens, w_up, w_down, task_heads, labels):
        n_tok, hidden = tokens.shape
        n_total = n_tok * n_data
        width = w_up.shape[1]
        n_task = task_heads.shape[0]
        blk = n_tok // n_model
        sub_blk = blk // 2
        half = width // 2
        win = -(-(hidden // 2) // LANES) * LANES
        off = hidden - win
        tile = 16 * sub_blk
        core = lax.axis_index('data')
        any_spec = pl.BlockSpec(memory_space=pl.ANY)
        vmem_spec = pl.BlockSpec(memory_space=pltpu.VMEM)
        heads = task_heads.astype(F32)
        d_row = heads[:, :, 0] - heads[:, :, 1]
        h_t = jnp.concatenate([task_heads[:, :, 0], task_heads[:, :, 1]], axis=0)
        h_win = lax.dynamic_slice(h_t, (0, core * off), (2 * n_task, win))
        col = lax.broadcasted_iota(jnp.int32, (2 * n_task, win), 1)
        edge = core * (win - hidden // 2)
        h_win = jnp.where((col >= edge) & (col < edge + hidden // 2), h_win, jnp.zeros_like(h_win))
        dma = pltpu.SemaphoreType.DMA
        vmem = pltpu.VMEM
        weights, grad_up, grad_down = pl.pallas_call(
            functools.partial(step_kernel, n_model, win, n_total),
            out_shape=(jax.ShapeDtypeStruct((8, LANES), F32), jax.ShapeDtypeStruct((hidden // 2, width), F32),
                       jax.ShapeDtypeStruct((half, hidden), F32)),
            in_specs=[any_spec, vmem_spec, vmem_spec, vmem_spec, vmem_spec, vmem_spec],
            out_specs=(vmem_spec, vmem_spec, vmem_spec),
            scratch_shapes=[vmem((2, tile, hidden), BF16), vmem((n_tok, width), BF16), vmem((width, n_tok), BF16),
                            vmem((width, n_tok), F32), vmem((2, 2, 4, sub_blk, 16 * width), BF16),
                            vmem((2, 16, half, win), BF16), vmem((2, blk, win), BF16),
                            vmem((24, sub_blk, win), F32), vmem((2, 2 * n_task, LANES), F32),
                            vmem((2, 2 * n_task, LANES), F32), vmem((2, n_task, LANES), F32),
                            vmem((2, n_model, n_task, LANES), F32),
                            vmem((n_task, width, hidden), F32), vmem((n_task * width, hidden), F32),
                            vmem((n_task, hidden, LANES), F32), vmem((n_task, 1, tile), F32), vmem((2 * width, tile), BF16),
                            vmem((1, LANES), F32), vmem((2 * n_model, 1, LANES), F32), vmem((win, width), F32),
                            dma((2,)), dma, dma((2, 4)), dma((2, 4, 2)), dma((2, 4, 2)), dma((3, 4)), dma((3, 4)),
                            dma((2, 4)), dma((2, 4)), dma((2,)), dma((2,)), dma((3,)), dma((3, n_task)),
                            dma((3, n_task)), dma, dma, pltpu.SemaphoreType.REGULAR],
            compiler_params=pltpu.CompilerParams(collective_id=0, has_side_effects=True, vmem_limit_bytes=67043328),
            name='step')(tokens, w_up.T, w_down, h_win, labels, d_row[:, None, :])
        return weights[0, :n_task], grad_up, grad_down

    return jax.shard_map(
        local_step, mesh=mesh,
        in_specs=(P('data', None), P(None, 'model'), P('model', None), P(None, None, None), P(None, 'data')),
        out_specs=(P(None), P('data', 'model'), P(('model', 'data'), None)),
        check_vma=False)
```

time: 1100 us -> 224 us (0.20)
  matrix products: 490 us -> 0 us
  waiting for transfers between devices: 473 us -> 0 us
  Pallas kernels: 0 us -> 213 us
  blocking collectives: 66.8 us -> 0 us
  other arithmetic: 28.6 us -> 2.16 us
  local copies, waits for them, and re-layouts: 22.1 us -> 7.72 us
  between operations: 14.9 us -> 0.67 us
    dot_general x10 -> x0, matrix products: 487 us -> none  [the longest x1 193 us: local_step(): jnp.einsum('tbc,tdc->tbd', dlogit, task_heads.astype(jnp.float32), precis...]
    psum x1 -> x0, waiting for transfers between devices: 465 us -> none  [local_step(): mlp_out = lax.psum(part_out, 'model')]
    pallas_call x0 -> x1, Pallas kernels: none -> 213 us  [local_step(): pl.pallas_call(functools.partial(step_kernel, n_model, win, n_total), out...]
    psum x1 -> x0, blocking collectives: 66.8 us -> none  [local_step(): gram_mat = lax.psum(gram_part, ('model', 'data'))]
    transpose x2 -> x0, local copies, waits for them, and re-layouts: 15.6 us -> none  [the longest x1 7.85 us: local_step(): jnp.einsum('bd,tbf->tdf', tokens, d_pre, preferred_element_type=jnp.float32)]
    reduce_sum x42 -> x0, other arithmetic: 15.4 us -> none  [the longest x20 12.4 us: eg_step(): return updated / jnp.sum(updated)]
    div x21 -> x0, other arithmetic: 13.1 us -> none  [the longest x20 13 us: eg_step(): return updated / jnp.sum(updated)]
  transfers between devices with their start and end apart: 3 -> 0, of which waited for: 2 -> 0; matrix products, arithmetic and copies ran while one was open for 13% -> 0% of each run, Pallas kernels for 0% -> 0%
where the time goes in v4:
time: 224 us; the launch traced here: 223 us
  Pallas kernels  213 us (95%)
  local copies, waits for them, and re-layouts  7.72 us (3%)
    pallas_call x1, Pallas kernels, local_step(): pl.pallas_call(functools.partial(step_kernel, n_model, win, n_total), out...  213 us
    unnamed x3, local copies, waits for them, and re-layouts  5.55 us

profile of v4, /device:TPU:1, one launch (start us, length us, event | category | flops | bytes accessed | tf_op | source)
XLA Modules:
  0.0 223.1 jit_solution(6174312690351207427)
XLA Ops:
  0.6 0.8 convert_element_type.3
  1.5 0.7 fusion.drow_ref
  2.2 1.0 fusion.4
  3.2 0.6 fusion.2.ht_ref
  3.8 2.0 copy.8
  5.8 212.6 %step.1 = (f32[8,128]{1,0:T(8,128)}, f32[832,128]{1,0:T(8,128)}, f32[64,1664]{1,0:T(8,128)}) custom-call(bf16[8192,1664]{1,0:T(8,128)(2,1)} %x_ref.1, bf16[128,1664]{1,0:T(8,128)(2,1)} %bitcast.9, bf16[128,1664]{1,0:T(8,128)(2,1)} %w2_ref.1, bf16[16,896]{1,0:T(8,128)(2,1)} %fusion.2.ht_ref, s32[8,8192]{1,0:T(8,128)} %lab_ref.1, f32[8,1,1664]{2,1,0:T(1,128)} %fusion.drow_ref), custom_call_target="tpu_custom_call" | custom-call | tf_op jit(solution)/shard_map/step/pallas_call | solution.py:574
  218.4 1.2 slice_bitcast_fusion
  219.6 1.8 copy.17
  221.4 1.8 copy.18
  (2 shorter events, 0.0 us)

commit v5 on v4

--- a/solution.py
+++ b/solution.py
@@ -21,24 +21,27 @@
     return {"model": model, "data": data}
 
 
-def step_kernel(n_model, win, n_total, x_ref, w1t_ref, w2_ref, ht_ref, lab_ref, drow_ref, a_ref, g1_ref, g2_ref,
-                xbuf, usend, ut_s, gp_s, uslab, wslab, xz, zall, lsend, lrecv, esend, et,
+def step_kernel(n_model, win, n_total, x_ref, w1_ref, w2_ref, h_ref, lab_ref, a_ref, g1_ref, g2_ref,
+                w1t_ref, ht_ref, drow_ref, xbuf, usend, ut_s, gp_s, uslab, wslab, xz, zall, lown, lsend, lrecv, esend, et,
                 dn_acc, up_acc, dcol, ebr, dat, msend, mrecv, g1t,
                 xsem, usend_sem, urecv_sem, wsend_sem, wrecv_sem, psend_sem, precv_sem, zsend_sem, zrecv_sem,
-                esend_sem, erecv_sem, lsem, gsend_sem, grecv_sem, msend_sem, mrecv_sem, free_sem):
+                esend_sem, erecv_sem, ssend_sem, srecv_sem, lsem, gsend_sem, grecv_sem, msend_sem, mrecv_sem, free_sem):
     me = lax.axis_index("model")
     core = lax.axis_index("data")
     ring = 4
     plane = ring * ring
     n_tok, hidden = x_ref.shape
     blk = n_tok // n_model
-    sub_blk = blk // 2
-    width = w1t_ref.shape[0]
+    n_part = 4
+    sub_blk = blk // n_part
+    width = w1_ref.shape[1]
     half = width // 2
     n_task = lab_ref.shape[0]
     off = hidden - win
-    tile = plane * sub_blk
-    n_tile = 2 * ring
+    tile = 2 * plane * sub_blk
+    n_tile = 2 * n_part
+    n_pair = n_task // 2
+    n_slot = n_part * 8
     n_all = 2 * n_model
     slot_of_me = me * 2 + core
     px, py, pz = lax.rem(me, ring), lax.rem(lax.div(me, ring), ring), lax.div(me, plane)
@@ -68,19 +71,19 @@
     lax.fori_loop(1, n_all, tell, 0)
 
     def block_of(j, k):
-        sub = lax.rem(j, ring)
+        sub = lax.rem(2 * j + lax.div(k, plane), ring)
         shift = jnp.where(sub == 0, 2, jnp.where(sub == 1, 1, jnp.where(sub == 2, 3, 0)))
-        return lax.rem(group + k, plane) * ring + lax.rem(px + shift, ring)
+        return lax.rem(group + lax.rem(k, plane), plane) * ring + lax.rem(px + shift, ring)
 
     def fetch(j, slot):
         def one(k, carry):
-            row = block_of(j, k) * blk + lax.div(j, ring) * sub_blk
+            row = block_of(j, k) * blk + lax.div(j, 2) * sub_blk
             pltpu.make_async_copy(x_ref.at[pl.ds(pl.multiple_of(row, sub_blk), sub_blk), :],
                                   xbuf.at[slot, pl.ds(pl.multiple_of(k * sub_blk, sub_blk), sub_blk), :],
                                   xsem.at[slot]).start()
             return carry
 
-        lax.fori_loop(0, plane, one, 0)
+        lax.fori_loop(0, 2 * plane, one, 0)
 
     def fetched(slot):
         pltpu.make_async_copy(xbuf.at[slot], xbuf.at[slot], xsem.at[slot]).wait()
@@ -122,6 +125,13 @@
     hw = [(h, way) for h in range(2) for way in range(2)]
     dn_acc[...] = jnp.zeros_like(dn_acc)
     up_acc[...] = jnp.zeros_like(up_acc)
+    w1t_ref[...] = w1_ref[...].T
+    first = core * (win - hidden // 2)
+    col = lax.broadcasted_iota(jnp.int32, (2 * n_task, win), 1)
+    h_rows = jnp.concatenate([h_ref[t, c:c + 1, w_cols].astype(F32) for c in range(2) for t in range(n_task)], axis=0)
+    ht_ref[...] = jnp.where((col >= first) & (col < first + hidden // 2), h_rows, 0.0).astype(BF16)
+    for t in range(n_task):
+        drow_ref[t] = h_ref[t, 0:1, :].astype(F32) - h_ref[t, 1:2, :].astype(F32)
 
     def spread(t, carry):
         dcol[t] = jnp.broadcast_to(drow_ref[t], (LANES, hidden)).T
@@ -129,7 +139,7 @@
 
     lax.fori_loop(0, n_task, spread, 0)
     pl.semaphore_wait(sem, n_all - 1)
-    far_x = remote(x_ref.at[mine, far_cols], xz.at[1], psend_sem.at[2, 0], precv_sem.at[2, 0], partner)
+    far_x = remote(x_ref.at[mine, far_cols], xz.at[1], lsem.at[3], lsem.at[4], partner)
     for h, way in hw:
         gather_copy(h, 0, way).start()
     far_x.start()
@@ -157,10 +167,9 @@
         return carry
 
     def give(n, carry):
-        j = lax.div(n, plane)
-        k = lax.rem(n, plane)
-        part, sub = lax.div(j, ring), lax.rem(j, ring)
-        g = lax.rem(group + k, plane)
+        run = lax.div(n, plane)
+        part, sub = lax.div(run, ring), lax.rem(run, ring)
+        g = lax.rem(group + lax.rem(n, plane), plane)
         src = usend.at[pl.ds(pl.multiple_of(n * sub_blk, sub_blk), sub_blk), :]
         dst = uslab.at[part, 0, sub, :, pl.ds(pl.multiple_of(group * width, width), width)]
 
@@ -173,12 +182,16 @@
             pltpu.make_async_copy(src, dst, urecv_sem.at[part, sub]).start()
         return carry
 
+    def give_part(part):
+        lax.fori_loop(part * (ring * plane), (part + 1) * (ring * plane), give, 0)
+
     lax.fori_loop(0, 1, forward, 0)
-    lax.fori_loop(0, plane, give, 0)
+    lax.fori_loop(0, 2 * plane, give, 0)
     for h, way in hw:
         gather_copy(h, 0, way).wait_recv()
         gather_copy(h, 1, way).start()
     lax.fori_loop(1, 2, forward, 0)
+    lax.fori_loop(2 * plane, 4 * plane, give, 0)
     for c in own:
         c.wait()
     for h, way in hw:
@@ -190,7 +203,7 @@
     for h, way in hw:
         gather_copy(h, 2, way).wait_recv()
         gather_copy(h, 3, way).start()
-    lax.fori_loop(plane, ring * plane, give, 0)
+    give_part(1)
 
     def u_pair(part, s):
         return remote(uslab.at[part, 0, s], uslab.at[part, 1, s], psend_sem.at[part, s], precv_sem.at[part, s], partner)
@@ -201,13 +214,13 @@
         u_pair(part, s).start()
 
     def z_out(part, n, q):
-        return part * 6 + n * 2 + q
+        return part * 8 + n * 2 + q
 
     def z_relay(part, q):
-        return 12 + part * 2 + q
+        return n_slot + part * 2 + q
 
     def z_in(part, i, q):
-        return 16 + part * 4 + i * 2 + q
+        return n_slot + 2 * n_part + part * 4 + i * 2 + q
 
     def z_copy(part, n):
         left, right = at(px - 1, py, pz), at(px + 1, py, pz)
@@ -221,74 +234,71 @@
         y, z = g % ring, g // ring
         return [(0, z * ring + y), (1, y * ring + z)]
 
-    def partial_z(part, s, put):
+    def partial_z(part, subs, relayed):
         for c in range(0, win, wide):
             size = min(wide, win - c)
-            total = jnp.zeros((2 * sub_blk, size), F32)
+            total = jnp.zeros((2 * len(subs) * sub_blk, size), F32)
             for g in range(0, plane, 2):
                 left = jnp.concatenate(
-                    [uslab[part, q, s, :, g * width:(g + 2) * width] for q in range(2)], axis=0)
+                    [uslab[part, q, s, :, g * width:(g + 2) * width] for s in subs for q in range(2)], axis=0)
                 right = jnp.concatenate([wslab[h, i, :, c:c + size] for h, i in rows_of(g) + rows_of(g + 1)], axis=0)
                 total = total + jnp.dot(left, right, preferred_element_type=F32)
-            put(c, size, total[:sub_blk], total[sub_blk:])
-
-    def z_far(part):
-        u_pair(part, 0).wait_recv()
-
-        def put(c, size, top, low):
-            zall[z_out(part, 0, 0), :, c:c + size] = top
-            zall[z_out(part, 0, 1), :, c:c + size] = low
-
-        partial_z(part, 0, put)
+            for i, s in enumerate(subs):
+                for q in range(2):
+                    v = total[(2 * i + q) * sub_blk:(2 * i + q + 1) * sub_blk]
+                    if relayed and q == s - 1:
+                        v = v + zall[z_relay(part, q), :, c:c + size]
+                    zall[z_out(part, s, q), :, c:c + size] = v
+
+    def z_first(s):
+        u_pair(0, s).wait_recv()
+        if s in (1, 2):
+            z_copy(0, s - 1).wait_recv()
+        partial_z(0, (s,), True)
+        for n in ((0, 1), (2,), (3,), ())[s]:
+            z_copy(0, n).start()
+
+    def z_all(part):
+        for s in range(4):
+            u_pair(part, s).wait_recv()
+        partial_z(part, (0, 1, 2, 3), False)
         z_copy(part, 0).start()
         z_copy(part, 1).start()
 
-    def z_near(part, s):
-        u_pair(part, s).wait_recv()
-        z_copy(part, s - 1).wait_recv()
-
-        def put(c, size, top, low):
-            for q, v in enumerate((top, low)):
-                if q == s - 1:
-                    v = v + zall[z_relay(part, q), :, c:c + size]
-                zall[z_out(part, s, q), :, c:c + size] = v
-
-        partial_z(part, s, put)
-        z_copy(part, s + 1).start()
-
-    def z_own(part):
-        u_pair(part, 3).wait_recv()
-        z_copy(part, 0).wait_send()
-        z_copy(part, 1).wait_send()
-
-        def put(c, size, top, low):
-            zall[z_out(part, 0, 0), :, c:c + size] = top
-            zall[z_out(part, 0, 1), :, c:c + size] = low
-
-        partial_z(part, 3, put)
-
-    pad = jnp.zeros((n_task, LANES - sub_blk), F32)
-
-    def e_out(part):
+    def z_relay_on(part):
+        for q in range(2):
+            z_copy(part, q).wait_recv()
+            zall[z_out(part, 1 + q, q)] += zall[z_relay(part, q)]
+            z_copy(part, 2 + q).start()
+
+    pad = jnp.zeros((n_task, blk - sub_blk), F32)
+
+    def swap(part):
+        return remote(lsend.at[part], lrecv.at[part], ssend_sem.at[part], srecv_sem.at[part], partner)
+
+    def e_logits(part):
         z_copy(part, 2).wait_recv()
         z_copy(part, 3).wait_recv()
-        z_copy(part, 2).wait_send()
-        z_copy(part, 3).wait_send()
+        for n in range(4):
+            z_copy(part, n).wait_send()
         gaps = []
-        rows = slice(part * sub_blk, (part + 1) * sub_blk)
+        rows = pl.ds(pl.multiple_of(part * sub_blk, sub_blk), sub_blk)
         for q in range(2):
-            z = (xz[q, rows, :].astype(F32) + ((zall[z_out(part, 0, q)] + zall[z_in(part, 0, q)]) + zall[z_in(part, 1, q)])).astype(BF16)
+            z = (xz[q, rows, :].astype(F32) + ((zall[z_out(part, 3, q)] + zall[z_in(part, 0, q)])
+                                               + zall[z_in(part, 1, q)])).astype(BF16)
             gaps.append(lax.dot_general(ht_ref[...], z, NT, preferred_element_type=F32))
-        lsend[part] = jnp.concatenate([gaps[1], jnp.concatenate([pad, pad], axis=0)], axis=1)
-        swap = remote(lsend.at[part], lrecv.at[part], psend_sem.at[2, 1 + part], precv_sem.at[2, 1 + part], partner)
-        swap.start()
-        swap.wait()
-        logit = gaps[0] + lrecv[part, :, :sub_blk]
+        both = jnp.concatenate([pad, pad], axis=0)
+        lown[part] = jnp.concatenate([gaps[0], both], axis=1)
+        lsend[part] = jnp.concatenate([gaps[1], both], axis=1)
+        swap(part).start()
+
+    def e_out(part):
+        swap(part).wait()
+        logit = lown[part] + lrecv[part]
         gap = logit[:n_task, :] - logit[n_task:, :]
-        first = lab_ref[:, mine][:, rows] == 0
-        wrong = 1.0 / (1.0 + jnp.exp(jnp.where(first, gap, -gap)))
-        e = jnp.where(first, -wrong, wrong) * (1.0 / n_total)
-        esend[part] = jnp.concatenate([e, pad], axis=1)
+        first_class = pltpu.roll(lab_ref[:, mine], lax.rem(blk - part * sub_blk, blk), 1) == 0
+        wrong = 1.0 / (1.0 + jnp.exp(jnp.where(first_class, gap, -gap)))
+        esend[part] = jnp.where(first_class, -wrong, wrong) * (1.0 / n_total)
         dst = et.at[part, me]
 
         def send(k, carry):
@@ -302,20 +312,20 @@
     def e_in(part):
         pltpu.make_async_copy(et.at[part], et.at[part], erecv_sem.at[part]).wait()
 
-    u_arrive(0, 0)
+    def u_in(part):
+        for s in range(4):
+            u_arrive(part, s)
+
+    u_in(0)
     for h, way in hw:
         gather_copy(h, 3, way).wait_recv()
-    z_far(0)
-    u_arrive(0, 1)
-    z_near(0, 1)
-    u_arrive(0, 2)
-    z_near(0, 2)
-    u_arrive(0, 3)
-    lax.fori_loop(ring * plane, n_tile * plane, give, 0)
+    for s in range(4):
+        z_first(s)
+    u_in(1)
     far_x.wait_recv()
-    z_own(0)
+    e_logits(0)
     e_out(0)
-    e_in(0)
+    z_all(1)
 
     def far_down(t):
         rows = pl.ds(pl.multiple_of(lax.rem(t, 2) * half, half), half)
@@ -324,10 +334,10 @@
     def grad_copies(t):
         out = [remote(dn_acc.at[t, pl.ds(pl.multiple_of((1 - core) * half, half), half), :], far_down(t),
                       gsend_sem.at[0, t], grecv_sem.at[0, t], partner)]
-        for i in range(2):
-            rows = pl.ds(pl.multiple_of(t * width + i * half, half), half)
-            out.append(remote(up_acc.at[rows, far_cols], zall.at[2 * t + i],
-                              gsend_sem.at[1 + i, t], grecv_sem.at[1 + i, t], partner))
+        for i in range(n_part):
+            rows = pl.ds(pl.multiple_of(t * width + i * sub_blk, sub_blk), sub_blk)
+            out.append(remote(up_acc.at[rows, far_cols], zall.at[n_part * t + i],
+                              gsend_sem.at[1, t], grecv_sem.at[1, t], partner))
         return out
 
     def grad_tile(j, carry):
@@ -341,12 +351,17 @@
         def _():
             pl.semaphore_signal(free_sem, inc=1, device_id=partner, device_id_type=MESH)
 
-        part = lax.div(j, ring)
-        for k in range(0, plane, 2):
-            pieces = [et[part, block_of(j, k + i)][:, :sub_blk] for i in range(2)]
+        part = lax.div(j, 2)
+
+        @pl.when(lax.rem(j, 2) == 0)
+        def _():
+            e_in(part)
+
+        for k in range(0, 2 * plane, n_part):
+            pieces = [et[part, block_of(j, k + i)][:, :sub_blk] for i in range(n_part)]
             e_pair = jnp.concatenate(pieces, axis=1)
             for t in range(n_task):
-                ebr[t, :, k * sub_blk:(k + 2) * sub_blk] = e_pair[t:t + 1, :]
+                ebr[t, :, k * sub_blk:(k + n_part) * sub_blk] = e_pair[t:t + 1, :]
         fetched(slot)
         base = pl.multiple_of(j * tile, tile)
 
@@ -384,36 +399,45 @@
                 for q in range(2):
                     for c in grad_copies(2 * m + q):
                         c.start()
+            hook = lax.rem(j, 2) * n_pair + m
+            ahead = part + 1
+
+            @pl.when((hook == 0) & (ahead < n_part))
+            def _():
+                z_relay_on(ahead)
+
+            @pl.when((hook == 0) & (ahead + 1 < n_part))
+            def _():
+                give_part(ahead + 1)
+
+            @pl.when((hook == 3) & (ahead < n_part))
+            def _():
+                e_logits(ahead)
+
+            @pl.when((hook == 4) & (ahead < n_part))
+            def _():
+                e_out(ahead)
+
+            @pl.when((hook == 5) & (ahead + 1 < n_part))
+            def _():
+                u_in(ahead + 1)
+
+            @pl.when((hook == 6) & (ahead + 1 < n_part))
+            def _():
+                z_all(ahead + 1)
             return carry
 
-        lax.fori_loop(0, n_task // 2, pair_of_tasks, 0)
-
-        @pl.when(j == 0)
-        def _():
-            for s in range(4):
-                u_arrive(1, s)
-            z_far(1)
-
-        @pl.when(j == 1)
-        def _():
-            z_near(1, 1)
-            z_near(1, 2)
-            z_own(1)
-
-        @pl.when(j == 2)
-        def _():
-            e_out(1)
-
-        @pl.when(j == 3)
-        def _():
-            e_in(1)
+        lax.fori_loop(0, n_pair, pair_of_tasks, 0)
         return carry
 
     lax.fori_loop(0, n_tile, grad_tile, 0)
 
+    def up_slots(t):
+        return zall.at[pl.ds(pl.multiple_of(n_part * t, n_part), n_part)]
+
     def landed(t, carry):
-        for c in grad_copies(t):
-            c.wait_recv()
+        grad_copies(t)[0].wait_recv()
+        pltpu.make_async_copy(up_slots(t), up_slots(t), grecv_sem.at[1, t]).wait()
         return carry
 
     lax.fori_loop(0, n_task, landed, 0)
@@ -437,25 +461,25 @@
             sums = gram_of(vals, sums)
         return sums
 
-    first = core * (win - hidden // 2)
-
-    def fold_up(i, r, sums):
+    n_row = sub_blk // 8
+
+    def fold_up(n, sums):
+        i, r = lax.div(n, n_row), lax.rem(n, n_row)
         rows = pl.ds(pl.multiple_of(r * 8, 8), 8)
         for c in range(0, win, LANES):
             edge = c < win - hidden // 2 or c + LANES > hidden // 2
             vals = []
             for t in range(n_task):
-                v = up_acc[pl.ds(pl.multiple_of(t * width + i * half + r * 8, 8), 8),
-                           pl.ds(pl.multiple_of(core * off + c, LANES), LANES)] + zall[2 * t + i, rows, c:c + LANES]
-                zall[2 * t + i, rows, c:c + LANES] = v
+                v = up_acc[pl.ds(pl.multiple_of(t * width + n * 8, 8), 8),
+                           pl.ds(pl.multiple_of(core * off + c, LANES), LANES)] + zall[n_part * t + i, rows, c:c + LANES]
+                zall[n_part * t + i, rows, c:c + LANES] = v
                 vals.append(jnp.where((lane + c >= first) & (lane + c < first + hidden // 2), v, 0.0) if edge else v)
             sums = gram_of(vals, sums)
         return sums
 
     sums = tuple(jnp.zeros((8, LANES), F32) for _ in pairs)
     sums = lax.fori_loop(0, half // 8, fold_down, sums)
-    for i in range(2):
-        sums = lax.fori_loop(0, half // 8, functools.partial(fold_up, i), sums)
+    sums = lax.fori_loop(0, width // 8, fold_up, sums)
     lane1 = lax.broadcasted_iota(jnp.int32, (1, LANES), 1)
     row = lax.broadcasted_iota(jnp.int32, (8, LANES), 0)
     out = jnp.zeros((1, LANES), F32)
@@ -507,26 +531,26 @@
 
     last = z_in(0, 0, 0)
 
-    def mix_up(i, r, carry):
+    def mix_up(n, carry):
+        i, r = lax.div(n, n_row), lax.rem(n, n_row)
         rows = pl.ds(pl.multiple_of(r * 8, 8), 8)
         for c in range(0, win, LANES):
             total = a[0] * zall[i, rows, c:c + LANES]
             for t in range(1, n_task):
-                total = total + a[t] * zall[2 * t + i, rows, c:c + LANES]
+                total = total + a[t] * zall[n_part * t + i, rows, c:c + LANES]
             zall[last + i, rows, c:c + LANES] = total
         return carry
 
     lax.fori_loop(0, half // 8, mix_down, 0)
-    for i in range(2):
-        lax.fori_loop(0, half // 8, functools.partial(mix_up, i), 0)
+    lax.fori_loop(0, width // 8, mix_up, 0)
     for c in range(0, win, LANES):
-        g1t[c:c + LANES, :] = jnp.concatenate([zall[last + i, :, c:c + LANES] for i in range(2)], axis=0).T
+        g1t[c:c + LANES, :] = jnp.concatenate([zall[last + i, :, c:c + LANES] for i in range(n_part)], axis=0).T
     g1_ref[...] = g1t[pl.ds(pl.multiple_of(first, 8), hidden // 2), :]
 
     for h, way in hw:
         for stage in range(4):
             gather_copy(h, stage, way).wait_send()
-    for part in range(2):
+    for part in range(n_part):
         for s in range(4):
             u_pair(part, s).wait_send()
         sent = et.at[part, pl.ds(0, n_model - 1)]
@@ -536,8 +560,8 @@
     pltpu.make_async_copy(sent, sent, usend_sem).wait()
 
     def gone(t, carry):
-        for c in grad_copies(t):
-            c.wait_send()
+        grad_copies(t)[0].wait_send()
+        pltpu.make_async_copy(up_slots(t), up_slots(t), gsend_sem.at[1, t]).wait()
         return carry
 
     lax.fori_loop(0, n_task, gone, 0)
@@ -554,43 +578,35 @@
         width = w_up.shape[1]
         n_task = task_heads.shape[0]
         blk = n_tok // n_model
-        sub_blk = blk // 2
+        sub_blk = blk // 4
         half = width // 2
         win = -(-(hidden // 2) // LANES) * LANES
-        off = hidden - win
-        tile = 16 * sub_blk
-        core = lax.axis_index('data')
+        tile = 32 * sub_blk
         any_spec = pl.BlockSpec(memory_space=pl.ANY)
         vmem_spec = pl.BlockSpec(memory_space=pltpu.VMEM)
-        heads = task_heads.astype(F32)
-        d_row = heads[:, :, 0] - heads[:, :, 1]
-        h_t = jnp.concatenate([task_heads[:, :, 0], task_heads[:, :, 1]], axis=0)
-        h_win = lax.dynamic_slice(h_t, (0, core * off), (2 * n_task, win))
-        col = lax.broadcasted_iota(jnp.int32, (2 * n_task, win), 1)
-        edge = core * (win - hidden // 2)
-        h_win = jnp.where((col >= edge) & (col < edge + hidden // 2), h_win, jnp.zeros_like(h_win))
         dma = pltpu.SemaphoreType.DMA
         vmem = pltpu.VMEM
         weights, grad_up, grad_down = pl.pallas_call(
             functools.partial(step_kernel, n_model, win, n_total),
             out_shape=(jax.ShapeDtypeStruct((8, LANES), F32), jax.ShapeDtypeStruct((hidden // 2, width), F32),
                        jax.ShapeDtypeStruct((half, hidden), F32)),
-            in_specs=[any_spec, vmem_spec, vmem_spec, vmem_spec, vmem_spec, vmem_spec],
+            in_specs=[any_spec, vmem_spec, vmem_spec, vmem_spec, vmem_spec],
             out_specs=(vmem_spec, vmem_spec, vmem_spec),
-            scratch_shapes=[vmem((2, tile, hidden), BF16), vmem((n_tok, width), BF16), vmem((width, n_tok), BF16),
-                            vmem((width, n_tok), F32), vmem((2, 2, 4, sub_blk, 16 * width), BF16),
+            scratch_shapes=[vmem((width, hidden), BF16), vmem((2 * n_task, win), BF16), vmem((n_task, 1, hidden), F32),
+                            vmem((2, tile, hidden), BF16), vmem((n_tok, width), BF16), vmem((width, n_tok), BF16),
+                            vmem((width, n_tok), F32), vmem((4, 2, 4, sub_blk, 16 * width), BF16),
                             vmem((2, 16, half, win), BF16), vmem((2, blk, win), BF16),
-                            vmem((24, sub_blk, win), F32), vmem((2, 2 * n_task, LANES), F32),
-                            vmem((2, 2 * n_task, LANES), F32), vmem((2, n_task, LANES), F32),
-                            vmem((2, n_model, n_task, LANES), F32),
+                            vmem((56, sub_blk, win), F32), vmem((4, 2 * n_task, blk), F32),
+                            vmem((4, 2 * n_task, blk), F32), vmem((4, 2 * n_task, blk), F32),
+                            vmem((4, n_task, blk), F32), vmem((4, n_model, n_task, blk), F32),
                             vmem((n_task, width, hidden), F32), vmem((n_task * width, hidden), F32),
                             vmem((n_task, hidden, LANES), F32), vmem((n_task, 1, tile), F32), vmem((2 * width, tile), BF16),
                             vmem((1, LANES), F32), vmem((2 * n_model, 1, LANES), F32), vmem((win, width), F32),
-                            dma((2,)), dma, dma((2, 4)), dma((2, 4, 2)), dma((2, 4, 2)), dma((3, 4)), dma((3, 4)),
-                            dma((2, 4)), dma((2, 4)), dma((2,)), dma((2,)), dma((3,)), dma((3, n_task)),
-                            dma((3, n_task)), dma, dma, pltpu.SemaphoreType.REGULAR],
+                            dma((2,)), dma, dma((4, 4)), dma((2, 4, 2)), dma((2, 4, 2)), dma((4, 4)), dma((4, 4)),
+                            dma((4, 4)), dma((4, 4)), dma((4,)), dma((4,)), dma((4,)), dma((4,)), dma((5,)),
+                            dma((2, n_task)), dma((2, n_task)), dma, dma, pltpu.SemaphoreType.REGULAR],
             compiler_params=pltpu.CompilerParams(collective_id=0, has_side_effects=True, vmem_limit_bytes=67043328),
-            name='step')(tokens, w_up.T, w_down, h_win, labels, d_row[:, None, :])
+            name='step')(tokens, w_up, w_down, jnp.transpose(task_heads, (0, 2, 1)), labels)
         return weights[0, :n_task], grad_up, grad_down
 
     return jax.shard_map(

time: 224 us -> 213 us (0.951)
  Pallas kernels: 213 us -> 207 us
  local copies, waits for them, and re-layouts: 7.72 us -> 4.78 us
    pallas_call x1, Pallas kernels: 213 us -> 207 us  [local_step(): pl.pallas_call(functools.partial(step_kernel, n_model, win, n_total), out...]
    unnamed x3 -> x2, local copies, waits for them, and re-layouts: 5.55 us -> 3.58 us
where the time goes in v5:
time: 213 us
  Pallas kernels  207 us (97%)
  local copies, waits for them, and re-layouts  4.78 us (2%)
    pallas_call x1, Pallas kernels, local_step(): pl.pallas_call(functools.partial(step_kernel, n_model, win, n_total), out...  207 us

profile of v5, /device:TPU:1, one launch (start us, length us, event | category | flops | bytes accessed | tf_op | source)
XLA Modules:
  0.0 212.9 jit_solution(16003367585288170964)
XLA Ops:
  0.6 207.5 %step.1 = (f32[8,128]{1,0:T(8,128)}, f32[832,128]{1,0:T(8,128)}, f32[64,1664]{1,0:T(8,128)}) custom-call(bf16[8192,1664]{1,0:T(8,128)(2,1)} %x_ref.1, bf16[1664,128]{1,0:T(8,128)(2,1)} %w1_ref.1, bf16[128,1664]{1,0:T(8,128)(2,1)} %w2_ref.1, bf16[8,2,1664]{2,1,0:T(2,128)(2,1)} %bitcast.3, s32[8,8192]{1,0:T(8,128)} %lab_ref.1), custom_call_target="tpu_custom_call" | custom-call | tf_op jit(solution)/shard_map/step/pallas_call | solution.py:589
  208.1 1.2 slice_bitcast_fusion
  209.3 1.8 copy.10
  211.1 1.8 copy.11

commit v6 on v5

--- a/solution.py
+++ b/solution.py
@@ -40,7 +40,8 @@
     off = hidden - win
     tile = 2 * plane * sub_blk
     n_tile = 2 * n_part
-    n_pair = n_task // 2
+    body_tasks = 4
+    n_body = n_task // body_tasks
     n_slot = n_part * 8
     n_all = 2 * n_model
     slot_of_me = me * 2 + core
@@ -58,9 +59,13 @@
         return pltpu.make_async_remote_copy(src_ref=src, dst_ref=dst, send_sem=ssem, recv_sem=rsem,
                                             device_id=dev, device_id_type=MESH)
 
+    def chip(k):
+        z, y, x = [lax.rem(lax.div(k, n), ring) for n in (plane, ring, 1)]
+        z, y, x = [jnp.where(v == 0, 2, jnp.where(v == 1, 1, jnp.where(v == 2, 3, 0))) for v in (z, y, x)]
+        return (lax.rem(pz + z, ring) * plane + lax.rem(py + y, ring) * ring + lax.rem(px + x, ring))
+
     def other(k):
-        dev = lax.rem(slot_of_me + k, n_all)
-        return peer(lax.div(dev, 2), lax.rem(dev, 2))
+        return peer(chip(lax.div(k, 2)), lax.rem(core + 1 + lax.rem(k, 2), 2))
 
     sem = pltpu.get_barrier_semaphore()
 
@@ -68,7 +73,7 @@
         pl.semaphore_signal(sem, inc=1, device_id=other(k), device_id_type=MESH)
         return carry
 
-    lax.fori_loop(1, n_all, tell, 0)
+    lax.fori_loop(0, n_all - 1, tell, 0)
 
     def block_of(j, k):
         sub = lax.rem(2 * j + lax.div(k, plane), ring)
@@ -303,10 +308,10 @@
 
         def send(k, carry):
             remote(esend.at[part], dst, esend_sem.at[part], erecv_sem.at[part],
-                   peer(lax.rem(me + k, n_model), core)).start()
+                   peer(chip(k), core)).start()
             return carry
 
-        lax.fori_loop(1, n_model, send, 0)
+        lax.fori_loop(0, n_model - 1, send, 0)
         pltpu.make_async_copy(esend.at[part], dst, erecv_sem.at[part]).start()
 
     def e_in(part):
@@ -321,11 +326,13 @@
         gather_copy(h, 3, way).wait_recv()
     for s in range(4):
         z_first(s)
-    u_in(1)
     far_x.wait_recv()
     e_logits(0)
     e_out(0)
+    u_in(1)
     z_all(1)
+    give_part(2)
+    z_relay_on(1)
 
     def far_down(t):
         rows = pl.ds(pl.multiple_of(lax.rem(t, 2) * half, half), half)
@@ -365,10 +372,10 @@
         fetched(slot)
         base = pl.multiple_of(j * tile, tile)
 
-        def pair_of_tasks(m, carry):
-            rows = pl.ds(pl.multiple_of(2 * m * width, 2 * width), 2 * width)
-            for q in range(2):
-                t = 2 * m + q
+        def some_tasks(m, carry):
+            rows = pl.ds(pl.multiple_of(body_tasks * m * width, body_tasks * width), body_tasks * width)
+            for q in range(body_tasks):
+                t = body_tasks * m + q
                 for n in range(0, tile, wide):
                     n_size = min(wide, tile)
                     e_n = ebr[t, :, n:n + n_size]
@@ -379,13 +386,23 @@
                         da = da + jnp.dot(w2_ref[:, c:c + size], dz_t, preferred_element_type=F32)
                     cols = pl.ds(pl.multiple_of(base + n, n_size), n_size)
                     dat[q * width:(q + 1) * width, n:n + n_size] = (da * gp_s[:, cols]).astype(BF16)
-            for q in range(2):
-                t = 2 * m + q
-                e_col = jnp.broadcast_to(ebr[t], (LANES, tile)).T
-                for c, size in cuts:
-                    e_b = jnp.concatenate([e_col] * (size // LANES), axis=1)
-                    dz = (e_b * drow_ref[t, :, c:c + size]).astype(BF16)
-                    dn_acc[t, :, c:c + size] += jnp.dot(ut_s[:, pl.ds(base, tile)], dz, preferred_element_type=F32)
+            left = ut_s[:, pl.ds(base, tile)]
+            for q in range(0, body_tasks, 2):
+                ts = (body_tasks * m + q, body_tasks * m + q + 1)
+                e_col = [jnp.broadcast_to(ebr[t], (LANES, tile)).T for t in ts]
+                for i, t in enumerate(ts):
+                    for c, size in cuts:
+                        if size == wide:
+                            e_b = jnp.concatenate([e_col[i]] * (size // LANES), axis=1)
+                            dz = (e_b * drow_ref[t, :, c:c + size]).astype(BF16)
+                            dn_acc[t, :, c:c + size] += jnp.dot(left, dz, preferred_element_type=F32)
+                c, size = cuts[-1]
+                if size < wide:
+                    dz = jnp.concatenate([e_col[i] * drow_ref[t, :, c:c + size] for i, t in enumerate(ts)],
+                                         axis=1).astype(BF16)
+                    both = jnp.dot(left, dz, preferred_element_type=F32)
+                    for i, t in enumerate(ts):
+                        dn_acc[t, :, c:c + size] += both[:, i * size:(i + 1) * size]
             left = dat[...]
             for c, size in cuts:
                 up_acc[rows, c:c + size] += jnp.dot(left, xbuf[slot, :, c:c + size], preferred_element_type=F32)
@@ -396,38 +413,38 @@
 
             @pl.when(j == n_tile - 1)
             def _():
-                for q in range(2):
-                    for c in grad_copies(2 * m + q):
+                for q in range(body_tasks):
+                    for c in grad_copies(body_tasks * m + q):
                         c.start()
-            hook = lax.rem(j, 2) * n_pair + m
+            hook = lax.rem(j, 2) * n_body + m
             ahead = part + 1
 
             @pl.when((hook == 0) & (ahead < n_part))
             def _():
-                z_relay_on(ahead)
-
-            @pl.when((hook == 0) & (ahead + 1 < n_part))
-            def _():
-                give_part(ahead + 1)
-
-            @pl.when((hook == 3) & (ahead < n_part))
-            def _():
                 e_logits(ahead)
 
-            @pl.when((hook == 4) & (ahead < n_part))
+            @pl.when((hook == 1) & (ahead < n_part))
             def _():
                 e_out(ahead)
 
-            @pl.when((hook == 5) & (ahead + 1 < n_part))
+            @pl.when((hook == 1) & (ahead + 1 < n_part))
             def _():
                 u_in(ahead + 1)
 
-            @pl.when((hook == 6) & (ahead + 1 < n_part))
+            @pl.when((hook == 2) & (ahead + 1 < n_part))
             def _():
                 z_all(ahead + 1)
+
+            @pl.when((hook == 2) & (ahead + 2 < n_part))
+            def _():
+                give_part(ahead + 2)
+
+            @pl.when((hook == 3) & (ahead + 1 < n_part))
+            def _():
+                z_relay_on(ahead + 1)
             return carry
 
-        lax.fori_loop(0, n_pair, pair_of_tasks, 0)
+        lax.fori_loop(0, n_body, some_tasks, 0)
         return carry
 
     lax.fori_loop(0, n_tile, grad_tile, 0)
@@ -492,7 +509,7 @@
         remote(msend, mrecv.at[slot_of_me], msend_sem, mrecv_sem, other(k)).start()
         return carry
 
-    lax.fori_loop(1, n_all, send_gram, 0)
+    lax.fori_loop(0, n_all - 1, send_gram, 0)
     pltpu.make_async_copy(msend, mrecv.at[slot_of_me], mrecv_sem).start()
     pltpu.make_async_copy(mrecv, mrecv, mrecv_sem).wait()
     flat = jnp.sum(mrecv[...], axis=0)
@@ -600,7 +617,7 @@
                             vmem((4, 2 * n_task, blk), F32), vmem((4, 2 * n_task, blk), F32),
                             vmem((4, n_task, blk), F32), vmem((4, n_model, n_task, blk), F32),
                             vmem((n_task, width, hidden), F32), vmem((n_task * width, hidden), F32),
-                            vmem((n_task, hidden, LANES), F32), vmem((n_task, 1, tile), F32), vmem((2 * width, tile), BF16),
+                            vmem((n_task, hidden, LANES), F32), vmem((n_task, 1, tile), F32), vmem((4 * width, tile), BF16),
                             vmem((1, LANES), F32), vmem((2 * n_model, 1, LANES), F32), vmem((win, width), F32),
                             dma((2,)), dma, dma((4, 4)), dma((2, 4, 2)), dma((2, 4, 2)), dma((4, 4)), dma((4, 4)),
                             dma((4, 4)), dma((4, 4)), dma((4,)), dma((4,)), dma((4,)), dma((4,)), dma((5,)),

time: 213 us -> 217 us (1.019)
  Pallas kernels: 207 us -> 211 us
    pallas_call x1, Pallas kernels: 207 us -> 211 us  [local_step(): pl.pallas_call(functools.partial(step_kernel, n_model, win, n_total), out...]
where the time goes in v6:
time: 217 us; the launch traced here: 216 us
  Pallas kernels  211 us (97%)
  local copies, waits for them, and re-layouts  4.78 us (2%)
    pallas_call x1, Pallas kernels, local_step(): pl.pallas_call(functools.partial(step_kernel, n_model, win, n_total), out...  211 us

profile of v6, /device:TPU:1, one launch (start us, length us, event | category | flops | bytes accessed | tf_op | source)
XLA Modules:
  0.0 216.3 jit_solution(1052957173881458206)
XLA Ops:
  0.6 210.9 %step.1 = (f32[8,128]{1,0:T(8,128)}, f32[832,128]{1,0:T(8,128)}, f32[64,1664]{1,0:T(8,128)}) custom-call(bf16[8192,1664]{1,0:T(8,128)(2,1)} %x_ref.1, bf16[1664,128]{1,0:T(8,128)(2,1)} %w1_ref.1, bf16[128,1664]{1,0:T(8,128)(2,1)} %w2_ref.1, bf16[8,2,1664]{2,1,0:T(2,128)(2,1)} %bitcast.3, s32[8,8192]{1,0:T(8,128)} %lab_ref.1), custom_call_target="tpu_custom_call" | custom-call | tf_op jit(solution)/shard_map/step/pallas_call | solution.py:606
  211.5 1.2 slice_bitcast_fusion
  212.7 1.8 copy.10
  214.5 1.8 copy.11

commit v7 on v6

--- a/solution.py
+++ b/solution.py
@@ -59,13 +59,9 @@
         return pltpu.make_async_remote_copy(src_ref=src, dst_ref=dst, send_sem=ssem, recv_sem=rsem,
                                             device_id=dev, device_id_type=MESH)
 
-    def chip(k):
-        z, y, x = [lax.rem(lax.div(k, n), ring) for n in (plane, ring, 1)]
-        z, y, x = [jnp.where(v == 0, 2, jnp.where(v == 1, 1, jnp.where(v == 2, 3, 0))) for v in (z, y, x)]
-        return (lax.rem(pz + z, ring) * plane + lax.rem(py + y, ring) * ring + lax.rem(px + x, ring))
-
     def other(k):
-        return peer(chip(lax.div(k, 2)), lax.rem(core + 1 + lax.rem(k, 2), 2))
+        dev = lax.rem(slot_of_me + k, n_all)
+        return peer(lax.div(dev, 2), lax.rem(dev, 2))
 
     sem = pltpu.get_barrier_semaphore()
 
@@ -73,7 +69,7 @@
         pl.semaphore_signal(sem, inc=1, device_id=other(k), device_id_type=MESH)
         return carry
 
-    lax.fori_loop(0, n_all - 1, tell, 0)
+    lax.fori_loop(1, n_all, tell, 0)
 
     def block_of(j, k):
         sub = lax.rem(2 * j + lax.div(k, plane), ring)
@@ -191,18 +187,19 @@
         lax.fori_loop(part * (ring * plane), (part + 1) * (ring * plane), give, 0)
 
     lax.fori_loop(0, 1, forward, 0)
-    lax.fori_loop(0, 2 * plane, give, 0)
+    lax.fori_loop(0, plane, give, 0)
     for h, way in hw:
         gather_copy(h, 0, way).wait_recv()
         gather_copy(h, 1, way).start()
+    lax.fori_loop(plane, 2 * plane, give, 0)
     lax.fori_loop(1, 2, forward, 0)
-    lax.fori_loop(2 * plane, 4 * plane, give, 0)
     for c in own:
         c.wait()
     for h, way in hw:
         gather_copy(h, 1, way).wait_recv()
     for h, way in hw:
         gather_copy(h, 2, way).start()
+    lax.fori_loop(2 * plane, 4 * plane, give, 0)
     lax.fori_loop(2, n_tile, forward, 0)
     fetch(0, 0)
     for h, way in hw:
@@ -308,10 +305,10 @@
 
         def send(k, carry):
             remote(esend.at[part], dst, esend_sem.at[part], erecv_sem.at[part],
-                   peer(chip(k), core)).start()
+                   peer(lax.rem(me + k, n_model), core)).start()
             return carry
 
-        lax.fori_loop(0, n_model - 1, send, 0)
+        lax.fori_loop(1, n_model, send, 0)
         pltpu.make_async_copy(esend.at[part], dst, erecv_sem.at[part]).start()
 
     def e_in(part):
@@ -331,8 +328,9 @@
     e_out(0)
     u_in(1)
     z_all(1)
+    e_in(0)
+    z_relay_on(1)
     give_part(2)
-    z_relay_on(1)
 
     def far_down(t):
         rows = pl.ds(pl.multiple_of(lax.rem(t, 2) * half, half), half)
@@ -360,7 +358,7 @@
 
         part = lax.div(j, 2)
 
-        @pl.when(lax.rem(j, 2) == 0)
+        @pl.when((lax.rem(j, 2) == 0) & (j > 0))
         def _():
             e_in(part)
 
@@ -509,7 +507,7 @@
         remote(msend, mrecv.at[slot_of_me], msend_sem, mrecv_sem, other(k)).start()
         return carry
 
-    lax.fori_loop(0, n_all - 1, send_gram, 0)
+    lax.fori_loop(1, n_all, send_gram, 0)
     pltpu.make_async_copy(msend, mrecv.at[slot_of_me], mrecv_sem).start()
     pltpu.make_async_copy(mrecv, mrecv, mrecv_sem).wait()
     flat = jnp.sum(mrecv[...], axis=0)

time: 217 us -> 210 us (0.968)
  Pallas kernels: 211 us -> 204 us
    pallas_call x1, Pallas kernels: 211 us -> 204 us  [local_step(): pl.pallas_call(functools.partial(step_kernel, n_model, win, n_total), out...]
where the time goes in v7:
time: 210 us; the launch traced here: 209 us
  Pallas kernels  204 us (97%)
  local copies, waits for them, and re-layouts  4.78 us (2%)
    pallas_call x1, Pallas kernels, local_step(): pl.pallas_call(functools.partial(step_kernel, n_model, win, n_total), out...  204 us

profile of v7, /device:TPU:1, one launch (start us, length us, event | category | flops | bytes accessed | tf_op | source)
XLA Modules:
  0.0 209.3 jit_solution(11080892327663812915)
XLA Ops:
  0.6 203.9 %step.1 = (f32[8,128]{1,0:T(8,128)}, f32[832,128]{1,0:T(8,128)}, f32[64,1664]{1,0:T(8,128)}) custom-call(bf16[8192,1664]{1,0:T(8,128)(2,1)} %x_ref.1, bf16[1664,128]{1,0:T(8,128)(2,1)} %w1_ref.1, bf16[128,1664]{1,0:T(8,128)(2,1)} %w2_ref.1, bf16[8,2,1664]{2,1,0:T(2,128)(2,1)} %bitcast.3, s32[8,8192]{1,0:T(8,128)} %lab_ref.1), custom_call_target="tpu_custom_call" | custom-call | tf_op jit(solution)/shard_map/step/pallas_call | solution.py:604
  204.5 1.2 slice_bitcast_fusion
  205.7 1.8 copy.10
  207.5 1.8 copy.11

commit v8 on v7

--- a/solution.py
+++ b/solution.py
@@ -23,7 +23,7 @@
 
 def step_kernel(n_model, win, n_total, x_ref, w1_ref, w2_ref, h_ref, lab_ref, a_ref, g1_ref, g2_ref,
                 w1t_ref, ht_ref, drow_ref, xbuf, usend, ut_s, gp_s, uslab, wslab, xz, zall, lown, lsend, lrecv, esend, et,
-                dn_acc, up_acc, dcol, ebr, dat, msend, mrecv, g1t,
+                dn_acc, up_acc, dcol, ebr, dat, msend, mrecv, g1s, g1t,
                 xsem, usend_sem, urecv_sem, wsend_sem, wrecv_sem, psend_sem, precv_sem, zsend_sem, zrecv_sem,
                 esend_sem, erecv_sem, ssend_sem, srecv_sem, lsem, gsend_sem, grecv_sem, msend_sem, mrecv_sem, free_sem):
     me = lax.axis_index("model")
@@ -60,16 +60,12 @@
                                             device_id=dev, device_id_type=MESH)
 
     def other(k):
-        dev = lax.rem(slot_of_me + k, n_all)
-        return peer(lax.div(dev, 2), lax.rem(dev, 2))
+        return peer(lax.rem(me + k // 2, n_model), 1 - core if k % 2 else core)
 
     sem = pltpu.get_barrier_semaphore()
 
-    def tell(k, carry):
+    for k in range(1, n_all):
         pl.semaphore_signal(sem, inc=1, device_id=other(k), device_id_type=MESH)
-        return carry
-
-    lax.fori_loop(1, n_all, tell, 0)
 
     def block_of(j, k):
         sub = lax.rem(2 * j + lax.div(k, plane), ring)
@@ -77,14 +73,13 @@
         return lax.rem(group + lax.rem(k, plane), plane) * ring + lax.rem(px + shift, ring)
 
     def fetch(j, slot):
-        def one(k, carry):
-            row = block_of(j, k) * blk + lax.div(j, 2) * sub_blk
-            pltpu.make_async_copy(x_ref.at[pl.ds(pl.multiple_of(row, sub_blk), sub_blk), :],
-                                  xbuf.at[slot, pl.ds(pl.multiple_of(k * sub_blk, sub_blk), sub_blk), :],
-                                  xsem.at[slot]).start()
-            return carry
-
-        lax.fori_loop(0, 2 * plane, one, 0)
+        for half_run in range(2):
+            first_block = block_of(j, half_run * plane) - group * ring
+            for k in range(plane):
+                row = (lax.rem(group + k, plane) * ring + first_block) * blk + lax.div(j, 2) * sub_blk
+                pltpu.make_async_copy(x_ref.at[pl.ds(pl.multiple_of(row, sub_blk), sub_blk), :],
+                                      xbuf.at[slot, pl.ds((half_run * plane + k) * sub_blk, sub_blk), :],
+                                      xsem.at[slot]).start()
 
     def fetched(slot):
         pltpu.make_async_copy(xbuf.at[slot], xbuf.at[slot], xsem.at[slot]).wait()
@@ -167,31 +162,28 @@
             usend[pl.ds(pl.multiple_of(base + n, step), step), :] = u_f.T.astype(BF16)
         return carry
 
-    def give(n, carry):
-        run = lax.div(n, plane)
+    def give(run, carry):
         part, sub = lax.div(run, ring), lax.rem(run, ring)
-        g = lax.rem(group + lax.rem(n, plane), plane)
-        src = usend.at[pl.ds(pl.multiple_of(n * sub_blk, sub_blk), sub_blk), :]
         dst = uslab.at[part, 0, sub, :, pl.ds(pl.multiple_of(group * width, width), width)]
-
-        @pl.when(g != group)
-        def _():
-            remote(src, dst, usend_sem, urecv_sem.at[part, sub], peer(g * ring + px, core)).start()
-
-        @pl.when(g == group)
-        def _():
-            pltpu.make_async_copy(src, dst, urecv_sem.at[part, sub]).start()
+        base = run * (plane * sub_blk)
+        for k in range(plane):
+            src = usend.at[pl.ds(pl.multiple_of(base + k * sub_blk, sub_blk), sub_blk), :]
+            if k == 0:
+                pltpu.make_async_copy(src, dst, urecv_sem.at[part, sub]).start()
+            else:
+                owner = lax.rem(group + k, plane) * ring + px
+                remote(src, dst, usend_sem, urecv_sem.at[part, sub], peer(owner, core)).start()
         return carry
 
     def give_part(part):
-        lax.fori_loop(part * (ring * plane), (part + 1) * (ring * plane), give, 0)
+        lax.fori_loop(part * ring, (part + 1) * ring, give, 0)
 
     lax.fori_loop(0, 1, forward, 0)
-    lax.fori_loop(0, plane, give, 0)
+    lax.fori_loop(0, 1, give, 0)
     for h, way in hw:
         gather_copy(h, 0, way).wait_recv()
         gather_copy(h, 1, way).start()
-    lax.fori_loop(plane, 2 * plane, give, 0)
+    lax.fori_loop(1, 2, give, 0)
     lax.fori_loop(1, 2, forward, 0)
     for c in own:
         c.wait()
@@ -199,7 +191,7 @@
         gather_copy(h, 1, way).wait_recv()
     for h, way in hw:
         gather_copy(h, 2, way).start()
-    lax.fori_loop(2 * plane, 4 * plane, give, 0)
+    lax.fori_loop(2, 4, give, 0)
     lax.fori_loop(2, n_tile, forward, 0)
     fetch(0, 0)
     for h, way in hw:
@@ -303,12 +295,9 @@
         esend[part] = jnp.where(first_class, -wrong, wrong) * (1.0 / n_total)
         dst = et.at[part, me]
 
-        def send(k, carry):
+        for k in range(1, n_model):
             remote(esend.at[part], dst, esend_sem.at[part], erecv_sem.at[part],
                    peer(lax.rem(me + k, n_model), core)).start()
-            return carry
-
-        lax.fori_loop(1, n_model, send, 0)
         pltpu.make_async_copy(esend.at[part], dst, erecv_sem.at[part]).start()
 
     def e_in(part):
@@ -462,32 +451,35 @@
     def gram_of(vals, sums):
         return tuple(acc + vals[t] * vals[s] for acc, (t, s) in zip(sums, pairs))
 
+    n_row = sub_blk // 8
+
     def down_at(t, r, c):
         return (pl.ds(pl.multiple_of((t % 2) * half + r * 8, 8), 8), slice((t // 2) * hidden + c, (t // 2) * hidden + c + LANES))
 
+    def down_sum(t, r, c):
+        from_acc = pl.ds(pl.multiple_of(core * half + r * 8, 8), 8)
+        return dn_acc[t, from_acc, c:c + LANES] + gp_s[down_at(t, r, c)]
+
+    def up_sum(t, n, c):
+        rows = pl.ds(pl.multiple_of(lax.rem(n, n_row) * 8, 8), 8)
+        from_acc = pl.ds(pl.multiple_of(t * width + n * 8, 8), 8)
+        return (up_acc[from_acc, pl.ds(pl.multiple_of(core * off + c, LANES), LANES)]
+                + zall[n_part * t + lax.div(n, n_row), rows, c:c + LANES])
+
     def fold_down(r, sums):
-        from_acc = pl.ds(pl.multiple_of(core * half + r * 8, 8), 8)
         for c in range(0, hidden, LANES):
             vals = []
             for t in range(n_task):
-                v = dn_acc[t, from_acc, c:c + LANES] + gp_s[down_at(t, r, c)]
-                gp_s[down_at(t, r, c)] = v
-                vals.append(v)
+                vals.append(down_sum(t, r, c))
             sums = gram_of(vals, sums)
         return sums
 
-    n_row = sub_blk // 8
-
     def fold_up(n, sums):
-        i, r = lax.div(n, n_row), lax.rem(n, n_row)
-        rows = pl.ds(pl.multiple_of(r * 8, 8), 8)
         for c in range(0, win, LANES):
             edge = c < win - hidden // 2 or c + LANES > hidden // 2
             vals = []
             for t in range(n_task):
-                v = up_acc[pl.ds(pl.multiple_of(t * width + n * 8, 8), 8),
-                           pl.ds(pl.multiple_of(core * off + c, LANES), LANES)] + zall[n_part * t + i, rows, c:c + LANES]
-                zall[n_part * t + i, rows, c:c + LANES] = v
+                v = up_sum(t, n, c)
                 vals.append(jnp.where((lane + c >= first) & (lane + c < first + hidden // 2), v, 0.0) if edge else v)
             sums = gram_of(vals, sums)
         return sums
@@ -503,11 +495,8 @@
         out = out + jnp.where((lane1 == t * n_task + s) | (lane1 == s * n_task + t), total, 0.0)
     msend[...] = out
 
-    def send_gram(k, carry):
+    for k in range(1, n_all):
         remote(msend, mrecv.at[slot_of_me], msend_sem, mrecv_sem, other(k)).start()
-        return carry
-
-    lax.fori_loop(1, n_all, send_gram, 0)
     pltpu.make_async_copy(msend, mrecv.at[slot_of_me], mrecv_sem).start()
     pltpu.make_async_copy(mrecv, mrecv, mrecv_sem).wait()
     flat = jnp.sum(mrecv[...], axis=0)
@@ -535,31 +524,28 @@
     a = [jnp.broadcast_to(jnp.sum(jnp.where(lane == t, w, 0.0), axis=1, keepdims=True), (8, LANES))
          for t in range(n_task)]
 
+    def weigh(parts):
+        parts = [a[t] * v for t, v in enumerate(parts)]
+        while len(parts) > 1:
+            parts = [parts[i] + parts[i + 1] for i in range(0, len(parts), 2)]
+        return parts[0]
+
     def mix_down(r, carry):
         rows = pl.ds(pl.multiple_of(r * 8, 8), 8)
         for c in range(0, hidden, LANES):
-            total = a[0] * gp_s[down_at(0, r, c)]
-            for t in range(1, n_task):
-                total = total + a[t] * gp_s[down_at(t, r, c)]
-            g2_ref[rows, c:c + LANES] = total
-        return carry
-
-    last = z_in(0, 0, 0)
+            g2_ref[rows, c:c + LANES] = weigh([down_sum(t, r, c) for t in range(n_task)])
+        return carry
 
     def mix_up(n, carry):
-        i, r = lax.div(n, n_row), lax.rem(n, n_row)
-        rows = pl.ds(pl.multiple_of(r * 8, 8), 8)
+        rows = pl.ds(pl.multiple_of(n * 8, 8), 8)
         for c in range(0, win, LANES):
-            total = a[0] * zall[i, rows, c:c + LANES]
-            for t in range(1, n_task):
-                total = total + a[t] * zall[n_part * t + i, rows, c:c + LANES]
-            zall[last + i, rows, c:c + LANES] = total
+            g1s[rows, c:c + LANES] = weigh([up_sum(t, n, c) for t in range(n_task)])
         return carry
 
     lax.fori_loop(0, half // 8, mix_down, 0)
     lax.fori_loop(0, width // 8, mix_up, 0)
     for c in range(0, win, LANES):
-        g1t[c:c + LANES, :] = jnp.concatenate([zall[last + i, :, c:c + LANES] for i in range(n_part)], axis=0).T
+        g1t[c:c + LANES, :] = g1s[:, c:c + LANES].T
     g1_ref[...] = g1t[pl.ds(pl.multiple_of(first, 8), hidden // 2), :]
 
     for h, way in hw:
@@ -616,7 +602,7 @@
                             vmem((4, n_task, blk), F32), vmem((4, n_model, n_task, blk), F32),
                             vmem((n_task, width, hidden), F32), vmem((n_task * width, hidden), F32),
                             vmem((n_task, hidden, LANES), F32), vmem((n_task, 1, tile), F32), vmem((4 * width, tile), BF16),
-                            vmem((1, LANES), F32), vmem((2 * n_model, 1, LANES), F32), vmem((win, width), F32),
+                            vmem((1, LANES), F32), vmem((2 * n_model, 1, LANES), F32), vmem((width, win), F32), vmem((win, width), F32),
                             dma((2,)), dma, dma((4, 4)), dma((2, 4, 2)), dma((2, 4, 2)), dma((4, 4)), dma((4, 4)),
                             dma((4, 4)), dma((4, 4)), dma((4,)), dma((4,)), dma((4,)), dma((4,)), dma((5,)),
                             dma((2, n_task)), dma((2, n_task)), dma, dma, pltpu.SemaphoreType.REGULAR],

time: 210 us -> 198 us (0.943)
  Pallas kernels: 204 us -> 192 us
    pallas_call x1, Pallas kernels: 204 us -> 192 us  [local_step(): pl.pallas_call(functools.partial(step_kernel, n_model, win, n_total), out...]
where the time goes in v8:
time: 198 us
  Pallas kernels  192 us (97%)
  local copies, waits for them, and re-layouts  4.78 us (2%)
    pallas_call x1, Pallas kernels, local_step(): pl.pallas_call(functools.partial(step_kernel, n_model, win, n_total), out...  192 us

profile of v8, /device:TPU:1, one launch (start us, length us, event | category | flops | bytes accessed | tf_op | source)
XLA Modules:
  0.0 197.6 jit_solution(1229760326322179012)
XLA Ops:
  0.6 192.2 %step.1 = (f32[8,128]{1,0:T(8,128)}, f32[832,128]{1,0:T(8,128)}, f32[64,1664]{1,0:T(8,128)}) custom-call(bf16[8192,1664]{1,0:T(8,128)(2,1)} %x_ref.1, bf16[1664,128]{1,0:T(8,128)(2,1)} %w1_ref.1, bf16[128,1664]{1,0:T(8,128)(2,1)} %w2_ref.1, bf16[8,2,1664]{2,1,0:T(2,128)(2,1)} %bitcast.3, s32[8,8192]{1,0:T(8,128)} %lab_ref.1), custom_call_target="tpu_custom_call" | custom-call | tf_op jit(solution)/shard_map/step/pallas_call | solution.py:590
  192.9 1.2 slice_bitcast_fusion
  194.1 1.8 copy.10
  195.9 1.8 copy.11

commit v9 on v8

--- a/solution.py
+++ b/solution.py
@@ -400,9 +400,9 @@
 
             @pl.when(j == n_tile - 1)
             def _():
-                for q in range(body_tasks):
-                    for c in grad_copies(body_tasks * m + q):
-                        c.start()
+                copies = [grad_copies(body_tasks * m + q) for q in range(body_tasks)]
+                for c in [c[0] for c in copies] + [c for group_of in copies for c in group_of[1:]]:
+                    c.start()
             hook = lax.rem(j, 2) * n_body + m
             ahead = part + 1
 
@@ -439,12 +439,14 @@
     def up_slots(t):
         return zall.at[pl.ds(pl.multiple_of(n_part * t, n_part), n_part)]
 
-    def landed(t, carry):
+    def down_landed(t, carry):
         grad_copies(t)[0].wait_recv()
+        return carry
+
+    def up_landed(t, carry):
         pltpu.make_async_copy(up_slots(t), up_slots(t), grecv_sem.at[1, t]).wait()
         return carry
 
-    lax.fori_loop(0, n_task, landed, 0)
     pairs = [(t, s) for t in range(n_task) for s in range(t, n_task)]
     lane = lax.broadcasted_iota(jnp.int32, (8, LANES), 1)
 
@@ -485,7 +487,9 @@
         return sums
 
     sums = tuple(jnp.zeros((8, LANES), F32) for _ in pairs)
+    lax.fori_loop(0, n_task, down_landed, 0)
     sums = lax.fori_loop(0, half // 8, fold_down, sums)
+    lax.fori_loop(0, n_task, up_landed, 0)
     sums = lax.fori_loop(0, width // 8, fold_up, sums)
     lane1 = lax.broadcasted_iota(jnp.int32, (1, LANES), 1)
     row = lax.broadcasted_iota(jnp.int32, (8, LANES), 0)
@@ -510,16 +514,17 @@
 
     def eg_pair(i, w):
         v = jnp.sum(gram * w, axis=1, keepdims=True)
+        size = jnp.sum(w, axis=1, keepdims=True)
         w_col = jnp.sum(jnp.where(row == lane, w, 0.0), axis=1, keepdims=True)
-        w_col = w_col * jnp.exp(-v)
-        w_col = w_col / jnp.sum(w_col, axis=0, keepdims=True)
+        w_col = (w_col / size) * jnp.exp(-(v / size))
         v = jnp.sum(gram * w_col, axis=0, keepdims=True)
+        size = jnp.sum(w_col, axis=0, keepdims=True)
         w_row = jnp.sum(jnp.where(row == lane, w_col, 0.0), axis=0, keepdims=True)
-        w_row = w_row * jnp.exp(-v)
-        w_row = w_row / jnp.sum(w_row, axis=1, keepdims=True)
+        w_row = (w_row / size) * jnp.exp(-(v / size))
         return jnp.broadcast_to(w_row, (8, LANES))
 
     w = lax.fori_loop(0, STEPS // 2, eg_pair, w)
+    w = w / jnp.sum(w, axis=1, keepdims=True)
     a_ref[...] = w
     a = [jnp.broadcast_to(jnp.sum(jnp.where(lane == t, w, 0.0), axis=1, keepdims=True), (8, LANES))
          for t in range(n_task)]

time: 198 us -> 196 us (0.990)
  Pallas kernels: 192 us -> 190 us
    pallas_call x1, Pallas kernels: 192 us -> 190 us  [local_step(): pl.pallas_call(functools.partial(step_kernel, n_model, win, n_total), out...]
where the time goes in v9:
time: 196 us
  Pallas kernels  190 us (97%)
  local copies, waits for them, and re-layouts  4.78 us (2%)
    pallas_call x1, Pallas kernels, local_step(): pl.pallas_call(functools.partial(step_kernel, n_model, win, n_total), out...  190 us

profile of v9, /device:TPU:1, one launch (start us, length us, event | category | flops | bytes accessed | tf_op | source)
XLA Modules:
  0.0 195.6 jit_solution(3165670631997721635)
XLA Ops:
  0.6 190.2 %step.1 = (f32[8,128]{1,0:T(8,128)}, f32[832,128]{1,0:T(8,128)}, f32[64,1664]{1,0:T(8,128)}) custom-call(bf16[8192,1664]{1,0:T(8,128)(2,1)} %x_ref.1, bf16[1664,128]{1,0:T(8,128)(2,1)} %w1_ref.1, bf16[128,1664]{1,0:T(8,128)(2,1)} %w2_ref.1, bf16[8,2,1664]{2,1,0:T(2,128)(2,1)} %bitcast.3, s32[8,8192]{1,0:T(8,128)} %lab_ref.1), custom_call_target="tpu_custom_call" | custom-call | tf_op jit(solution)/shard_map/step/pallas_call | solution.py:595
  190.8 1.2 slice_bitcast_fusion
  192.0 1.8 copy.10
  193.8 1.8 copy.11
